TPU v7x, 32 devices: a 4x4x1 block of a 4x4x8 slice. The times are simulated.
32 devices in a mesh: rep: 1 (over z), r: 4 (over y), s: 8 (over x, core).
Axes of the slice: x: 4, y: 4, z: 1, core: 2. Of those that a mesh axis runs over, the one named last changes fastest.
The devices are a block of a 4x4x8 slice.
Arguments:
- x: bfloat16 [32, 2048, 1024], P(('rep', 'r', 's'))
- dy: bfloat16 [32, 2048, 1024], P(('rep', 'r', 's'))
- w_gate: bfloat16 [2, 1024, 3584], P(None, 's')
- w_up: bfloat16 [2, 1024, 3584], P(None, 's')
- w_down: bfloat16 [2, 3584, 1024], P(None, 's')
Outputs:
- output 1: bfloat16 [32, 2048, 1024], P(('rep', 'r', 's'))
- output 2: bfloat16 [2, 1024, 3584], P('rep', 's')
- output 3: bfloat16 [2, 1024, 3584], P('rep', 's')
- output 4: bfloat16 [2, 3584, 1024], P('rep', 's')
All inputs are finite; a program needn't handle non-finite values.
Results may differ from a plain program's by a relative error of at most 0.018.
Values are sent between devices in bfloat16 or wider.
A program may use at most 768 MiB of HBM per device.

v0:
```python
import jax
import jax.numpy as jnp
from jax import lax
from jax.sharding import PartitionSpec as P

NAMES = ("w_gate", "w_up", "w_down")


def matmul(a, w):
    return jnp.dot(a, w, preferred_element_type=jnp.float32).astype(jnp.bfloat16)


def normed(h):
    wide = h.astype(jnp.float32)
    scale = lax.rsqrt(jnp.mean(wide**2, -1, keepdims=True) + 1e-6)
    return (wide * scale).astype(jnp.bfloat16)


def layer(h, w):
    a = normed(h)
    gate = jnp.dot(a, w["w_gate"], preferred_element_type=jnp.float32)
    up = jnp.dot(a, w["w_up"], preferred_element_type=jnp.float32)
    return h + matmul((jax.nn.silu(gate) * up).astype(jnp.bfloat16), w["w_down"])


def solution(mesh):
    def fetched(weights, number):
        return {name: lax.all_gather(w[number], "s", axis=0, tiled=True) for name, w in zip(NAMES, weights, strict=True)}

    def summed(term):
        return lax.psum(lax.psum_scatter(term, "s", scatter_dimension=0, tiled=True), "r")

    def step(x, dy, *weights):
        layers = weights[0].shape[0]
        h, inputs = x[0], []
        for number in range(layers):
            inputs.append(h)
            h = layer(h, fetched(weights, number))
        by_h, mine = dy[0], [None] * layers
        for number in reversed(range(layers)):
            _, back = jax.vjp(lambda w, h: layer(h, w), fetched(weights, number), inputs[number])
            by_w, by_h = back(by_h)
            mine[number] = [summed(by_w[name]) for name in NAMES]
        return (by_h[None], *(jnp.stack([mine[number][i] for number in range(layers)]) for i in range(3)))

    states, cut = P(("rep", "r", "s"), None, None), P(None, "s", None)
    return jax.shard_map(
        step,
        mesh=mesh,
        in_specs=(states, states) + (cut,) * 3,
        out_specs=(states,) + (P("rep", "s", None),) * 3,
        check_vma=False,
    )
```

profile of v0, /device:TPU:97, one launch (start us, length us, event | category | flops | bytes accessed | tf_op | source)
XLA Modules:
  0.0 802.0 jit_solution(540332822085247866)
XLA Ops:
  7.3 2.9 fusion.68
  10.3 2.8 fusion.69
  13.2 0.1 all-gather.17.cloned.1.call-start
  13.3 1.4 fusion.70
  14.8 0.6 all-gather.21.cloned.1.call-update
  15.4 0.6 all-gather.23.cloned.1.call-update
  16.1 0.6 all-gather.19.cloned.1.call-update
  16.7 6.4 copy.10
  23.2 3.1 fusion.15
  26.2 0.6 copy-done.6
  26.8 6.5 copy.9
  33.3 23.9 %all-gather.13.cloned.1.call-done = bf16[1,1024,3584]{2,1,0:T(8,128)(2,1)} async-done(((bf16[1,128,3584]{2,1,0:T(8,128)(2,1)}), bf16[1,1024,3584]{2,1,0:T(8,128)(2,1)}) %all-gather.13.cloned.1.call-update) | async-done | bytes 7340048 | tf_op jit(solution)/shard_map/all_gather | solution.py:28
  57.2 24.3 %fusion.40 = f32[2048,3584]{1,0:T(8,128)} fusion(bf16[1,1024,3584]{2,1,0:T(8,128)(2,1)} %all-gather.13.cloned.1.call-done, bf16[1,2048,1024]{1,2,0:T(8,128)(2,1)} %copy.10, f32[2048]{0:T(1024)S(1)} %fusion.61), kind=kOutput, calls=%fused_computation.65 | convolution fusion | flops 15038676992 | bytes 40902656 | tf_op jit(solution)/shard_map/dot_general | solution.py:21
  81.5 20.0 %all-gather.15.cloned.1.call-done = bf16[1,1024,3584]{2,1,0:T(8,128)(2,1)} async-done(((bf16[1,128,3584]{2,1,0:T(8,128)(2,1)}), bf16[1,1024,3584]{2,1,0:T(8,128)(2,1)}) %all-gather.15.cloned.1.call-update) | async-done | bytes 7340048 | tf_op jit(solution)/shard_map/all_gather | solution.py:28
  101.5 34.8 %multiply_convert_fusion.1 = (bf16[2048,3584]{1,0:T(8,128)(2,1)}, f32[2048,3584]{1,0:T(8,128)}) fusion(f32[2048,3584]{1,0:T(8,128)} %fusion.40, bf16[1,1024,3584]{2,1,0:T(8,128)(2,1)} %all-gather.15.cloned.1.call-done, bf16[1,2048,1024]{1,2,0:T(8,128)(2,1)} %copy.10, f32[2048]{0:T(1024)S(1)} %fusion.61), kind=kOutput, calls=%fused_computation.13 | convolution fusion | flops 15082717184 | bytes 84942848 | tf_op jit(solution)/shard_map/dot_general | solution.py:22
  136.3 9.5 %all-gather.17.cloned.1.call-done = bf16[1,3584,1024]{2,1,0:T(8,128)(2,1)} async-done(((bf16[1,448,1024]{2,1,0:T(8,128)(2,1)}), bf16[1,3584,1024]{2,1,0:T(8,128)(2,1)}) %all-gather.17.cloned.1.call-update) | async-done | bytes 7340048 | tf_op jit(solution)/shard_map/all_gather | solution.py:28
  145.8 22.0 %fusion.18 = (f32[2048]{0:T(1024)S(1)}, bf16[2048,1024]{0,1:T(8,128)(2,1)}) fusion(bf16[2048,3584]{1,0:T(8,128)(2,1)} %get-tuple-element.20, bf16[1,3584,1024]{2,1,0:T(8,128)(2,1)} %all-gather.17.cloned.1.call-done, bf16[1,2048,1024]{1,2,0:T(8,128)(2,1)} %copy.10), kind=kOutput, calls=%fused_computation.40 | convolution fusion | flops 15042869248 | bytes 30416896 | tf_op jit(solution)/shard_map/dot_general | solution.py:10
  167.8 0.6 copy-done.12
  168.5 21.6 %all-gather.21.cloned.1.call-done = bf16[1,3584,1024]{2,1,0:T(8,128)(2,1)} async-done(((bf16[1,448,1024]{2,1,0:T(8,128)(2,1)}), bf16[1,3584,1024]{2,1,0:T(8,128)(2,1)}) %all-gather.21.cloned.1.call-update) | async-done | bytes 7340048 | tf_op jit(solution)/shard_map/all_gather | solution.py:28
  190.0 22.3 %convolution_convert_fusion.1 = bf16[2048,3584]{1,0:T(8,128)(2,1)} fusion(bf16[1,3584,1024]{2,1,0:T(8,128)(2,1)} %all-gather.21.cloned.1.call-done, bf16[1,2048,1024]{2,1,0:T(8,128)(2,1)} %param.6), kind=kOutput, calls=%fused_computation.21 | convolution fusion | flops 15039725568 | bytes 26214400 | tf_op jit(solution)/shard_map/transpose(jvp())/dot_general | solution.py:10
  212.3 22.5 %all-gather.23.cloned.1.call-done = bf16[1,1024,3584]{2,1,0:T(8,128)(2,1)} async-done(((bf16[1,128,3584]{2,1,0:T(8,128)(2,1)}), bf16[1,1024,3584]{2,1,0:T(8,128)(2,1)}) %all-gather.23.cloned.1.call-update) | async-done | bytes 7340048 | tf_op jit(solution)/shard_map/all_gather | solution.py:28
  234.8 24.5 %fusion.24 = f32[2048,3584]{1,0:T(8,128)} fusion(bf16[1,1024,3584]{2,1,0:T(8,128)(2,1)} %all-gather.23.cloned.1.call-done, bf16[2048,1024]{0,1:T(8,128)(2,1)} %get-tuple-element.23, f32[2048]{0:T(1024)S(1)} %fusion.62), kind=kOutput, calls=%fused_computation.49 | convolution fusion | flops 15038676992 | bytes 40902656 | tf_op jit(solution)/shard_map/jvp()/dot_general | solution.py:22
  259.2 20.3 %all-gather.19.cloned.1.call-done = bf16[1,1024,3584]{2,1,0:T(8,128)(2,1)} async-done(((bf16[1,128,3584]{2,1,0:T(8,128)(2,1)}), bf16[1,1024,3584]{2,1,0:T(8,128)(2,1)}) %all-gather.19.cloned.1.call-update) | async-done | bytes 7340048 | tf_op jit(solution)/shard_map/all_gather | solution.py:28
  279.5 43.5 %fusion.1 = (bf16[2048,3584]{1,0:T(8,128)(2,1)}, f32[2048,3584]{1,0:T(8,128)}) fusion(f32[2048,3584]{1,0:T(8,128)} %fusion.24, bf16[2048,3584]{1,0:T(8,128)(2,1)} %convolution_convert_fusion.1, bf16[1,1024,3584]{2,1,0:T(8,128)(2,1)} %all-gather.19.cloned.1.call-done, bf16[2048,1024]{0,1:T(8,128)(2,1)} %get-tuple-element.23, f32[2048]{0:T(1024)S(1)} %fusion.62), kind=kOutput, calls=%fused_computation.7 | convolution fusion | flops 15126757376 | bytes 99622912 | tf_op jit(solution)/shard_map/jvp()/dot_general | solution.py:21
  323.0 24.3 %fusion.7 = bf16[2048,1024]{0,1:T(8,128)(2,1)} fusion(bf16[2048,3584]{1,0:T(8,128)(2,1)} %convolution_convert_fusion.1, bf16[1,1024,3584]{2,1,0:T(8,128)(2,1)} %all-gather.23.cloned.1.call-done, f32[2048,3584]{1,0:T(8,128)} %get-tuple-element.25), kind=kOutput, calls=%fused_computation.17 | convolution fusion | flops 15076425728 | bytes 55574528 | tf_op jit(solution)/shard_map/transpose(jvp())/dot_general | solution.py:22
  347.4 22.4 %fusion.20 = (f32[2048]{0:T(1024)S(1)}, bf16[2048,1024]{0,1:T(8,128)(2,1)}) fusion(bf16[2048,1024]{0,1:T(8,128)(2,1)S(1)} %copy-done.4, bf16[2048,1024]{0,1:T(8,128)(2,1)} %fusion.7, bf16[2048,3584]{1,0:T(8,128)(2,1)} %get-tuple-element.24, bf16[1,1024,3584]{2,1,0:T(8,128)(2,1)} %all-gather.19.cloned.1.call-done), kind=kOutput, calls=%fused_computation.42 | convolution fusion | flops 15042869248 | bytes 34611200 | tf_op jit(solution)/shard_map/transpose(jvp())/dot_general | solution.py:21
  369.7 4.9 fusion.44
  374.6 2.0 copy-done.1
  376.6 20.6 %convolution_convert_fusion.2 = bf16[3584,1024]{1,0:T(8,128)(2,1)} fusion(bf16[2048,3584]{1,0:T(8,128)(2,1)} %get-tuple-element.20, bf16[2048,1024]{0,1:T(8,128)(2,1)S(1)} %fusion.44), kind=kOutput, calls=%fused_computation.46 | convolution fusion | flops 15036055552 | bytes 26214400 | tf_op jit(solution)/shard_map/transpose(jvp())/dot_general | solution.py:10
  397.4 27.6 %fusion.21 = bf16[3584,1024]{1,0:T(8,128)(2,1)} fusion(f32[2048,3584]{1,0:T(8,128)} %fusion.24, bf16[1,2048,1024]{2,1,0:T(8,128)(2,1)} %param.6, f32[2048,3584]{1,0:T(8,128)} %get-tuple-element.25), kind=kOutput, calls=%fused_computation.43 | convolution fusion | flops 15080095744 | bytes 70254592 | tf_op jit(solution)/shard_map/transpose(jvp())/dot_general | solution.py:10
  425.0 0.1 reduce-scatter.11.cloned.1.call-start
  425.1 40.4 %fusion.3 = (bf16[2048,3584]{1,0:T(8,128)(2,1)}, bf16[2048,3584]{1,0:T(8,128)(2,1)}) fusion(f32[2048,3584]{1,0:T(8,128)} %fusion.40, f32[2048,3584]{1,0:T(8,128)} %get-tuple-element.21, bf16[2048,1024]{0,1:T(8,128)(2,1)} %copy-done.1, bf16[1,3584,1024]{2,1,0:T(8,128)(2,1)} %all-gather.17.cloned.1.call-done), kind=kOutput, calls=%fused_computation.9 | convolution fusion | flops 15127805952 | bytes 99614720 | tf_op jit(solution)/shard_map/transpose(jvp())/dot_general | solution.py:10
  465.5 25.8 %fusion.22 = bf16[1024,3584]{1,0:T(8,128)(2,1)} fusion(bf16[2048,3584]{1,0:T(8,128)(2,1)} %get-tuple-element.29, bf16[1,2048,1024]{1,2,0:T(8,128)(2,1)} %copy.10, f32[2048]{0:T(1024)S(1)} %copy-done.9, f32[2048,3584]{1,0:T(8,128)} %fusion.40), kind=kOutput, calls=%fused_computation.44 | convolution fusion | flops 15086387200 | bytes 55582720 | tf_op jit(solution)/shard_map/transpose(jvp())/dot_general | solution.py:22
  491.4 0.1 reduce-scatter.13.cloned.1.call-start
  491.4 26.1 %fusion.23 = bf16[1024,3584]{1,0:T(8,128)(2,1)} fusion(bf16[2048,3584]{1,0:T(8,128)(2,1)} %convolution_convert_fusion.1, bf16[2048,1024]{0,1:T(8,128)(2,1)} %get-tuple-element.23, f32[2048]{0:T(1024)S(1)} %copy-done.11, f32[2048,3584]{1,0:T(8,128)} %get-tuple-element.25), kind=kOutput, calls=%fused_computation.45 | convolution fusion | flops 15086387200 | bytes 55582720 | tf_op jit(solution)/shard_map/transpose(jvp())/dot_general | solution.py:22
  517.7 21.6 %convolution_convert_fusion.3 = bf16[1024,3584]{1,0:T(8,128)(2,1)} fusion(bf16[2048,3584]{1,0:T(8,128)(2,1)} %get-tuple-element.24, bf16[2048,1024]{0,1:T(8,128)(2,1)} %get-tuple-element.23, f32[2048]{0:T(1024)S(1)} %copy-done.11), kind=kOutput, calls=%fused_computation.47 | convolution fusion | flops 15038676992 | bytes 26222592 | tf_op jit(solution)/shard_map/transpose(jvp())/dot_general | solution.py:21
  539.4 0.1 reduce-scatter.7.cloned.1.call-start
  539.5 22.0 %convolution_convert_fusion.4 = bf16[1024,3584]{1,0:T(8,128)(2,1)} fusion(bf16[2048,3584]{1,0:T(8,128)(2,1)} %get-tuple-element.28, bf16[1,2048,1024]{1,2,0:T(8,128)(2,1)} %copy.10, f32[2048]{0:T(1024)S(1)} %copy-done.9), kind=kOutput, calls=%fused_computation.48 | convolution fusion | flops 15038676992 | bytes 26222592 | tf_op jit(solution)/shard_map/transpose(jvp())/dot_general | solution.py:21
  561.7 21.0 %reduce-scatter.13.cloned.1.call-done = bf16[128,3584]{1,0:T(8,128)(2,1)} async-done(((bf16[1024,3584]{1,0:T(8,128)(2,1)}), bf16[128,3584]{1,0:T(8,128)(2,1)}) %reduce-scatter.13.cloned.1.call-update) | async-done | bytes 917520 | tf_op jit(solution)/shard_map/reduce_scatter | solution.py:31
  582.7 47.0 %reduce-scatter.9.cloned.1.call-done = bf16[128,3584]{1,0:T(8,128)(2,1)} async-done(((bf16[1024,3584]{1,0:T(8,128)(2,1)}), bf16[128,3584]{1,0:T(8,128)(2,1)}) %reduce-scatter.9.cloned.1.call-update) | async-done | bytes 917520 | tf_op jit(solution)/shard_map/reduce_scatter | solution.py:31
  629.6 46.8 %reduce-scatter.7.cloned.1.call-done = bf16[128,3584]{1,0:T(8,128)(2,1)} async-done(((bf16[1024,3584]{1,0:T(8,128)(2,1)}), bf16[128,3584]{1,0:T(8,128)(2,1)}) %reduce-scatter.7.cloned.1.call-update) | async-done | bytes 917520 | tf_op jit(solution)/shard_map/reduce_scatter | solution.py:31
  676.5 24.3 %fusion.9 = bf16[2048,1024]{0,1:T(8,128)(2,1)} fusion(bf16[2048,3584]{1,0:T(8,128)(2,1)} %get-tuple-element.29, bf16[1,1024,3584]{2,1,0:T(8,128)(2,1)} %all-gather.15.cloned.1.call-done, f32[2048,3584]{1,0:T(8,128)} %fusion.40), kind=kOutput, calls=%fused_computation.19 | convolution fusion | flops 15076425728 | bytes 55574528 | tf_op jit(solution)/shard_map/transpose(jvp())/dot_general | solution.py:22
  700.9 21.1 %fusion.17 = (f32[2048]{0:T(1024)S(1)}, bf16[2048,1024]{0,1:T(8,128)(2,1)S(1)}) fusion(bf16[1,2048,1024]{1,2,0:T(8,128)(2,1)S(1)} %copy-done, bf16[2048,1024]{0,1:T(8,128)(2,1)} %fusion.9, bf16[2048,3584]{1,0:T(8,128)(2,1)} %get-tuple-element.28, bf16[1,1024,3584]{2,1,0:T(8,128)(2,1)} %all-gather.13.cloned.1.call-done), kind=kOutput, calls=%fused_computation.39 | convolution fusion | flops 15042869248 | bytes 34611200 | tf_op jit(solution)/shard_map/transpose(jvp())/dot_general | solution.py:21
  722.0 4.7 fusion.43
  726.8 6.4 copy.11
  733.2 54.9 %all-reduce.3.cloned.1.call-done = (bf16[1,128,3584]{2,1,0:T(8,128)(2,1)}, bf16[1,128,3584]{2,1,0:T(8,128)(2,1)}, bf16[1,128,3584]{2,1,0:T(8,128)(2,1)}, bf16[1,...) async-done(((bf16[1,128,3584]{2,1,0:T(8,128)(2,1)}, bf16[1,128,3584]{2,1,0:T(8,128)(2,1)}, bf16[1,128,3584]{2,1,0:T(8,128)(2,1)}, ...) | async-done | bytes 5505040 | tf_op jit(solution)/shard_map/psum | solution.py:31
  788.1 2.9 pad_maximum_fusion.2
  790.9 4.2 pad_maximum_fusion
  (51 shorter events, 1.2 us)
Async XLA Ops:
  7.2 6.1 copy-start.5
  7.2 50.0 %all-gather.13.cloned.1.call-start = ((), (), s32[]{:S(2)}) async-start(), calls=%async_computation.12 | async-start | bytes 8257536 | tf_op jit(solution)/shard_map/all_gather | solution.py:28
  10.2 91.3 %all-gather.15.cloned.1.call-start = ((), (), s32[]{:S(2)}) async-start(), calls=%async_computation.13 | async-start | bytes 8257536 | tf_op jit(solution)/shard_map/all_gather | solution.py:28
  13.2 132.7 %all-gather.17.cloned.1.call-start = ((), (), s32[]{:S(2)}) async-start(), calls=%async_computation.14 | async-start | bytes 8257536 | tf_op jit(solution)/shard_map/all_gather | solution.py:28
  14.7 175.3 %all-gather.21.cloned.1.call-start = ((), (), s32[]{:S(2)}) async-start(), calls=%async_computation.16 | async-start | bytes 8257536 | tf_op jit(solution)/shard_map/all_gather | solution.py:28
  15.4 219.4 %all-gather.23.cloned.1.call-start = ((), (), s32[]{:S(2)}) async-start(), calls=%async_computation.17 | async-start | bytes 8257536 | tf_op jit(solution)/shard_map/all_gather | solution.py:28
  16.0 263.5 %all-gather.19.cloned.1.call-start = ((), (), s32[]{:S(2)}) async-start(), calls=%async_computation.15 | async-start | bytes 8257536 | tf_op jit(solution)/shard_map/all_gather | solution.py:28
  16.7 544.9 %reduce-scatter.15.cloned.1.call-start = ((), (), s32[]{:S(2)}) async-start(), calls=%async_computation.10 | async-start | bytes 8257536 | tf_op jit(solution)/shard_map/reduce_scatter | solution.py:31
  26.2 0.6 copy-start.6
  26.8 74.7 %copy-start.8 = (f32[2048]{0:T(1024)}, f32[2048]{0:T(1024)S(1)}, u32[]{:S(2)}) copy-start(f32[2048]{0:T(1024)S(1)} %fusion.61) | copy-start | bytes 24580
  167.8 0.6 copy-start.12
  168.5 201.3 %copy-start.10 = (f32[2048]{0:T(1024)}, f32[2048]{0:T(1024)S(1)}, u32[]{:S(2)}) copy-start(f32[2048]{0:T(1024)S(1)} %fusion.62) | copy-start | bytes 24580
  323.0 24.3 %copy-start.4 = (bf16[2048,1024]{0,1:T(8,128)(2,1)S(1)}, bf16[2048,1024]{0,1:T(8,128)(2,1)}, u32[]{:S(2)}) copy-start(bf16[2048,1024]{0,1:T(8,128)(2,1)} %get-tuple-element.23) | copy-start | bytes 12582916
  347.3 22.4 %copy-start.13 = (f32[2048]{0:T(1024)S(1)}, f32[2048]{0:T(1024)}, u32[]{:S(2)}) copy-start(f32[2048]{0:T(1024)} %copy-done.12) | copy-start | bytes 24580
  347.4 22.4 %copy-start.3 = (bf16[1,2048,1024]{1,2,0:T(8,128)(2,1)S(1)}, bf16[1,2048,1024]{1,2,0:T(8,128)(2,1)}, u32[]{:S(2)}) copy-start(bf16[1,2048,1024]{1,2,0:T(8,128)(2,1)} %copy.9) | copy-start | bytes 12582916
  374.6 2.0 copy-start.1
  397.3 164.3 %reduce-scatter.17.cloned.1.call-start = ((), (), s32[]{:S(2)}) async-start(), calls=%async_computation.11 | async-start | bytes 8257536 | tf_op jit(solution)/shard_map/reduce_scatter | solution.py:31
  425.0 136.7 %reduce-scatter.11.cloned.1.call-start = ((), (), s32[]{:S(2)}) async-start(), calls=%async_computation.8 | async-start | bytes 8257536 | tf_op jit(solution)/shard_map/reduce_scatter | solution.py:31
  425.1 40.4 %copy-start.9 = (f32[2048]{0:T(1024)S(1)}, f32[2048]{0:T(1024)}, u32[]{:S(2)}) copy-start(f32[2048]{0:T(1024)} %copy-done.8) | copy-start | bytes 24580
  465.5 25.9 %copy-start.11 = (f32[2048]{0:T(1024)S(1)}, f32[2048]{0:T(1024)}, u32[]{:S(2)}) copy-start(f32[2048]{0:T(1024)} %copy-done.10) | copy-start | bytes 24580
  491.4 91.3 %reduce-scatter.13.cloned.1.call-start = ((), (), s32[]{:S(2)}) async-start(), calls=%async_computation.9 | async-start | bytes 8257536 | tf_op jit(solution)/shard_map/reduce_scatter | solution.py:31
  517.6 112.0 %reduce-scatter.9.cloned.1.call-start = ((), (), s32[]{:S(2)}) async-start(), calls=%async_computation.7 | async-start | bytes 8257536 | tf_op jit(solution)/shard_map/reduce_scatter | solution.py:31
  539.4 137.1 %reduce-scatter.7.cloned.1.call-start = ((), (), s32[]{:S(2)}) async-start(), calls=%async_computation.6 | async-start | bytes 8257536 | tf_op jit(solution)/shard_map/reduce_scatter | solution.py:31
  561.5 226.6 %all-reduce.3.cloned.1.call-start = ((), (), s32[]{:S(2)}) async-start(), calls=%async_computation.18 | async-start | bytes 11010048 | tf_op jit(solution)/shard_map/psum | solution.py:31
  676.5 24.3 %copy-start = (bf16[1,2048,1024]{1,2,0:T(8,128)(2,1)S(1)}, bf16[1,2048,1024]{1,2,0:T(8,128)(2,1)}, u32[]{:S(2)}) copy-start(bf16[1,2048,1024]{1,2,0:T(8,128)(2,1)} %copy.10) | copy-start | bytes 12582916
  700.9 21.2 %copy-start.7 = (f32[2048]{0:T(1024)S(1)}, f32[2048]{0:T(1024)}, u32[]{:S(2)}) copy-start(f32[2048]{0:T(1024)} %copy-done.6) | copy-start | bytes 24580
  700.9 21.2 %copy-start.2 = (bf16[2048,1024]{0,1:T(8,128)(2,1)S(1)}, bf16[2048,1024]{0,1:T(8,128)(2,1)}, u32[]{:S(2)}) copy-start(bf16[2048,1024]{0,1:T(8,128)(2,1)} %copy-done.1) | copy-start | bytes 12582916
Sparse Core Ops, SparseCore 0:
  10.4 46.7 all-gather.12
  58.8 42.6 all-gather.14
  103.1 42.6 all-gather.16
  147.3 42.6 all-gather.20
  192.0 42.6 all-gather.22
  236.8 42.6 all-gather.18
  397.4 44.2 reduce-scatter.14
  444.1 44.6 reduce-scatter.16
  491.5 44.2 reduce-scatter.10
  538.0 44.6 reduce-scatter.12
  585.0 44.6 reduce-scatter.8
  631.8 44.6 reduce-scatter.6
  679.3 108.7 all-reduce.2
where the time goes:
time: 810 us; the launch traced here: 802 us
  matrix products  448 us (55%)
  waiting for transfers between devices  290 us (36%)
  local copies, waits for them, and re-layouts  29.7 us (4%)
  other arithmetic  19.7 us (2%)
  between operations  14.5 us (2%)
    dot_general x6, matrix products, layer(): up = jnp.dot(a, w['w_up'], preferred_element_type=jnp.float32)  160 us
    dot_general x6, matrix products, layer(): gate = jnp.dot(a, w['w_gate'], preferred_element_type=jnp.float32)  155 us
    dot_general x5, matrix products, matmul(): jnp.dot(a, w, preferred_element_type=jnp.float32).astype(jnp.bfloat16)  133 us
    all_gather x6, waiting for transfers between devices, fetched(): lax.all_gather(w[number], 's', axis=0, tiled=True)  118 us
    reduce_scatter x6, waiting for transfers between devices, summed(): lax.psum_scatter(term, 's', scatter_dimension=0, tiled=True)  115 us
    psum x1, waiting for transfers between devices, summed(): lax.psum(lax.psum_scatter(term, 's', scatter_dimension=0, tiled=True), 'r')  54.9 us
    unnamed x31, local copies, waits for them, and re-layouts  22.5 us
  transfers between devices with their start and end apart: 13, of which 10 were waited for; matrix products, arithmetic and copies ran while one was open for 46% of the time, Pallas kernels for 0%

commit v1 on v0

v1 whole, which is shorter than its diff:
```python
import functools

import jax
import jax.numpy as jnp
from jax import lax
from jax.experimental import pallas as pl
from jax.experimental.pallas import tpu as pltpu
from jax.sharding import PartitionSpec as P

BF, F32 = jnp.bfloat16, jnp.float32
MESH = pl.DeviceIdType.MESH
CORES = 2
BW = 128
TILES = 4
G_, U_, D_ = 0, 1, 2


def dot(a, b, ca=1, cb=0):
    return lax.dot_general(a, b, (((ca,), (cb,)), ((), ())), preferred_element_type=F32)


def when(condition, f):
    if isinstance(condition, bool):
        if condition:
            f()
    else:
        pl.when(condition)(f)


def kernel(dims, x_ref, dy_ref, own,
           by_x, og, od, G, ST, PT, A0T, H1,
           a_nat, a_t, dyv, acc, wbuf, dgu, pt, stb,
           s_send, d_recv, own32, r32, l32, s_u1, s_pr, s_pl, u2r, u2l, ra, rb, rc, rd, v, ya, yb, yc, f_out,
           g_send, g_recv, w_sem, st_sem, pt_sem, ld_sem, rs_send, d_sem, x_sem, rc_sem, y_sem, o_sem, od_send, od_recv):
    nx, ny, C, T, D = dims
    TM = T // TILES
    N = 2 * C
    DR = D // (CORES * nx)
    HR, QR = DR // 2, DR // 4
    CW = nx * BW
    DH = D // 2

    s, y = lax.axis_index("s"), lax.axis_index("r")
    X, k = lax.div(s, CORES), lax.rem(s, CORES)
    at = lambda xx, kk: CORES * lax.rem(xx, nx) + kk
    right, left = {"s": at(X + 1, k)}, {"s": at(X + nx - 1, k)}
    sib = {"s": at(X, 1 - k)}
    up, down = {"r": lax.rem(y + 1, ny)}, {"r": lax.rem(y + ny - 1, ny)}

    barrier = pltpu.get_barrier_semaphore()
    for who in (right, left, sib, up, down):
        pl.semaphore_signal(barrier, inc=1, device_id=who, device_id_type=MESH)
    pl.semaphore_wait(barrier, 5)

    def remote(src, dst, ss, rs, who):
        return pltpu.make_async_remote_copy(src_ref=src, dst_ref=dst, send_sem=ss, recv_sem=rs, device_id=who, device_id_type=MESH)

    def arrived(dst, rs):
        pltpu.make_async_copy(dst, dst, rs).wait()

    pL, pR, pO = at(X + nx - 1, k), at(X + 1, k), at(X + 2, k)
    par = lax.rem(y, 2)
    mine, other = par * HR, (1 - par) * HR

    def rows(base, q):
        return pl.ds(pl.multiple_of(base + q * QR, QR), QR)

    def out_copy(t, n):
        full = pl.ds(0, DR)
        spec = {
            0: (None, rows(mine, 0), right), 1: (None, rows(mine, 1), right),
            2: (None, rows(mine, 1), left), 3: (None, rows(mine, 0), left),
            4: (pL, rows(mine, 0), right), 5: (pR, rows(mine, 1), left),
            6: (pL, rows(mine, 0), up), 7: (pR, rows(mine, 0), up), 8: (pO, rows(mine, 0), up),
            9: (pL, rows(mine, 1), down), 10: (pR, rows(mine, 1), down), 11: (pO, rows(mine, 1), down),
            12: (None, full, sib), 13: (pL, full, sib), 14: (pR, full, sib), 15: (pO, full, sib),
        }
        j, r, who = spec[t]
        src = own.at[n, :, r, :] if j is None else G.at[n, :, j, r, :]
        return remote(src, G.at[n, :, s if j is None else j, r, :], g_send.at[n, t], g_recv.at[n, t], who)

    def in_wait(t, n):
        full = pl.ds(0, DR)
        oL, oR, oO, oS = at(X + nx - 1, 1 - k), at(X + 1, 1 - k), at(X + 2, 1 - k), at(X, 1 - k)
        spec = {
            0: (pL, rows(mine, 0)), 1: (pL, rows(mine, 1)), 2: (pR, rows(mine, 1)), 3: (pR, rows(mine, 0)),
            4: (pO, rows(mine, 0)), 5: (pO, rows(mine, 1)),
            6: (pL, rows(other, 0)), 7: (pR, rows(other, 0)), 8: (pO, rows(other, 0)),
            9: (pL, rows(other, 1)), 10: (pR, rows(other, 1)), 11: (pO, rows(other, 1)),
            12: (oS, full), 13: (oL, full), 14: (oR, full), 15: (oO, full),
        }
        j, r = spec[t]
        arrived(G.at[n, :, j, r, :], g_recv.at[n, t])

    def stage(f):
        def run(n):
            when((n >= 0) & (n < N) if not isinstance(n, int) else 0 <= n < N, lambda: f(n))
        return run

    def starts(n, *ts):
        for t in ts:
            out_copy(t, n).start()

    @stage
    def gA(n):
        starts(n, 0, 2, 1, 3, 12)

    @stage
    def gB(n):
        in_wait(0, n)
        starts(n, 4, 6)
        in_wait(2, n)
        starts(n, 5, 10)

    @stage
    def gC(n):
        in_wait(1, n)
        starts(n, 9)
        in_wait(3, n)
        starts(n, 7)

    @stage
    def gD(n):
        in_wait(4, n)
        starts(n, 8)
        in_wait(5, n)
        starts(n, 11)

    @stage
    def gE(n):
        for a, b, t in ((6, 9, 13), (7, 10, 14), (8, 11, 15)):
            in_wait(a, n)
            in_wait(b, n)
            starts(n, t)

    def load_weights(n, slot):
        pltpu.make_async_copy(own.at[n], wbuf.at[slot, :, s], w_sem.at[slot]).start()
        for j in range(1, CORES * nx):
            p = lax.rem(s + j, CORES * nx)
            pltpu.make_async_copy(G.at[n, :, p], wbuf.at[slot, :, p], w_sem.at[slot]).start()

    def wait_weights(slot):
        pltpu.make_async_copy(wbuf.at[slot], wbuf.at[slot], w_sem.at[slot]).wait()

    @stage
    def gF(n):
        for t in (12, 13, 14, 15):
            in_wait(t, n)
        load_weights(n, lax.rem(n, 2))

    def w_cols(slot, q):
        return wbuf[slot, q].reshape(D, CW)

    def w_half(slot, q, h):
        return wbuf[slot, q, pl.ds(h * nx, nx)].reshape(DH, CW)

    def wd_half(slot, h):
        return jnp.concatenate([wbuf[slot, D_, CORES * j + h] for j in range(nx)], axis=0)

    def tile(i, n=None):
        n = TM if n is None else n
        return pl.ds(pl.multiple_of(i * n, n), n)

    def rel(j):
        return lax.rem(X + j, nx)

    def lane_lhs(lane):
        return jnp.concatenate([a_t[rel(j), lane] for j in range(nx)], axis=0)

    def grad(q, lane):
        if q == D_:
            lhs = jnp.concatenate([pt[rel(j)] for j in range(nx)], axis=0)
            return dot(lhs, dyv[lane])
        return dot(lane_lhs(lane), dgu[q])

    def d_copy(q, m):
        return remote(s_send.at[q], d_recv.at[lax.rem(m, 2), q], rs_send.at[q], d_sem.at[lax.rem(m, 2), q], sib)

    def send_lane(q, m):
        when(m > 0, lambda: d_copy(q, m).wait_send())
        s_send[q] = grad(q, 1 - k).astype(BF).reshape(nx, DR, CW)
        d_copy(q, m).start()

    lo, hi = pl.ds(0, HR), pl.ds(HR, HR)

    def x_copy(t, m):
        two, three = lax.rem(m, 2), lax.rem(m, 3)
        src, dst, sem, who = {
            0: (s_u1.at[:, lo], ra.at[two], x_sem.at[two, 0], right),
            1: (s_u1.at[:, hi], rb.at[two], x_sem.at[two, 1], left),
            2: (s_pr, rc.at[three, :, hi], rc_sem.at[three, 0], right),
            3: (s_pl, rd.at[three, :, lo], rc_sem.at[three, 1], left),
            4: (u2r, rc.at[three, :, lo], rc_sem.at[three, 2], right),
            5: (u2l, rd.at[three, :, hi], rc_sem.at[three, 3], left),
        }[t]
        return remote(src, dst, rs_send.at[3 + t], sem, who)

    def x_wait(t, m):
        two, three = lax.rem(m, 2), lax.rem(m, 3)
        dst, sem = {
            0: (ra.at[two], x_sem.at[two, 0]),
            1: (rb.at[two], x_sem.at[two, 1]),
            2: (rc.at[three, :, hi], rc_sem.at[three, 0]),
            3: (rd.at[three, :, lo], rc_sem.at[three, 1]),
            4: (rc.at[three, :, lo], rc_sem.at[three, 2]),
            5: (rd.at[three, :, hi], rc_sem.at[three, 3]),
        }[t]
        arrived(dst, sem)

    def y_copy(t, m):
        three = lax.rem(m, 3)
        src, dst, who = {
            0: (v.at[three, :, lo], ya.at[three, :, lo], up),
            1: (v.at[three, :, hi], ya.at[three, :, hi], up),
            2: (v.at[three, :, hi], yb.at[three, :, hi], down),
            3: (v.at[three, :, lo], yb.at[three, :, lo], down),
            4: (ya.at[three, :, lo], yc.at[three, :, lo], up),
            5: (yb.at[three, :, hi], yc.at[three, :, hi], down),
        }[t]
        return remote(src, dst, y_sem.at[0, three, t], y_sem.at[1, three, t], who)

    def y_wait(t, m):
        three = lax.rem(m, 3)
        dst = {0: ya.at[three, :, lo], 1: ya.at[three, :, hi], 2: yb.at[three, :, hi], 3: yb.at[three, :, lo],
               4: yc.at[three, :, lo], 5: yc.at[three, :, hi]}[t]
        arrived(dst, y_sem.at[1, three, t])

    def keep_lane(q, m):
        two = lax.rem(m, 2)
        arrived(d_recv.at[two, q], d_sem.at[two, q])
        total = (grad(q, k) + d_recv[two, q].reshape(CW, CW).astype(F32)).reshape(nx, DR, CW)
        own32[two, q] = total[0]
        r32[q] = total[1, :HR]
        s_pr[q] = total[1, HR:].astype(BF)
        s_u1[q] = total[2].astype(BF)
        s_pl[q] = total[3, :HR].astype(BF)
        l32[q] = total[3, HR:]

    def before_keep(m):
        def f():
            for t in range(4):
                x_copy(t, m - 1).wait_send()
        when(m > 0, f)

    def x1(m):
        for t in range(4):
            x_copy(t, m).start()

    def x2(m):
        x_wait(0, m)
        x_wait(1, m)

        def f():
            x_copy(4, m - 1).wait_send()
            x_copy(5, m - 1).wait_send()
        when(m > 0, f)
        two = lax.rem(m, 2)
        for q in range(3):
            u2r[q] = (r32[q] + ra[two, q].astype(F32)).astype(BF)
            u2l[q] = (l32[q] + rb[two, q].astype(F32)).astype(BF)
        x_copy(4, m).start()
        x_copy(5, m).start()

    def x3(m):
        for t in (2, 3, 4, 5):
            x_wait(t, m)
        two, three = lax.rem(m, 2), lax.rem(m, 3)
        for q in range(3):
            v[three, q] = (own32[two, q] + rc[three, q].astype(F32) + rd[three, q].astype(F32)).astype(BF)
        for t in range(4):
            y_copy(t, m).start()

    def y2(m):
        y_wait(0, m)
        y_copy(4, m).start()
        y_wait(2, m)
        y_copy(5, m).start()

    def where_m(m):
        first = m < C
        return jnp.where(first, 1, 0), jnp.where(first, m, m - C)

    def od_place(h):
        o = jnp.where(h >= C, 1, 0)
        return o, pl.ds(pl.multiple_of(HR * (h - C * o), HR), HR)

    def od_cols():
        return pl.ds(pl.multiple_of(k * DH, DH), DH)

    def og_copy(q, m):
        layer, c = where_m(m)
        return pltpu.make_async_copy(f_out.at[q], og.at[layer * C + c, q], o_sem.at[q])

    def od_each(m, local, far):
        layer, c = where_m(m)
        for e in range(2):
            o, r = od_place(2 * c + e)
            src, dst = f_out.at[D_, pl.ds(e * HR, HR)], od.at[layer, r, od_cols()]
            pl.when(o == k)(functools.partial(local, pltpu.make_async_copy(src, dst, o_sem.at[2 + e])))
            pl.when(o != k)(functools.partial(far, remote(src, dst, od_send.at[e], od_recv, sib)))

    def out_done(m):
        for q in (G_, U_):
            og_copy(q, m).wait()
        od_each(m, lambda c: c.wait(), lambda c: c.wait_send())

    def y3(m):
        for t in (1, 3, 4, 5):
            y_wait(t, m)
        when(m > 0, lambda: out_done(m - 1))
        three = lax.rem(m, 3)
        for q in range(3):
            a = v[three, q].astype(F32) + yc[three, q].astype(F32)
            b = ya[three, q].astype(F32) + yb[three, q].astype(F32)
            f_out[q] = (a + b).astype(BF)
        for t in range(6):
            y_copy(t, m).wait_send()
        for q in (G_, U_):
            og_copy(q, m).start()
        od_each(m, lambda c: c.start(), lambda c: c.start())

    def lagged(f, m):
        when(m >= 0, lambda: f(m))

    def halves(src, dst, r, sem):
        return [pltpu.make_async_copy(src.at[r, pl.ds(h * DH, DH)], dst.at[h, r], sem) for h in range(2)]

    every = pl.ds(0, T)
    for c_ in halves(x_ref.at[0], dyv, every, ld_sem.at[0]):
        c_.start()
    gA(0)
    pltpu.make_async_copy(dyv, dyv, ld_sem.at[0]).wait()

    NT = 2 * TILES
    TN = T // NT

    def both(ref, r):
        return jnp.concatenate([ref[0, r, :], ref[1, r, :]], axis=1)

    def put_a(h, i):
        r = tile(i, TN)
        scale = lax.rsqrt(jnp.mean(h * h, -1, keepdims=True) + 1e-6)
        a = (h * scale).astype(BF)
        a_nat[r, :] = a
        a_t[:, :, :, r] = a.T.reshape(nx, CORES, DR, TN)

    def norm0(i, _):
        r = tile(i, TN)
        put_a(both(dyv, r).astype(F32), i)
        acc[r, :] = jnp.zeros((TN, D), F32)
        return _

    lax.fori_loop(0, NT, norm0, 0)
    a0t_out = pltpu.make_async_copy(a_t, A0T, ld_sem.at[1])
    a0t_out.start()
    gB(0)
    gA(1)
    gC(0)
    gD(0)
    gB(1)
    gA(2)
    gC(1)
    gE(0)
    gD(1)
    gF(0)
    gB(2)
    gA(3)
    gC(2)
    gE(1)
    gD(2)

    def st_out(tau):
        return pltpu.make_async_copy(stb.at[lax.rem(tau, 2)], ST.at[tau], st_sem.at[lax.rem(tau, 2)])

    def pt_out(c, i):
        cols = tile(i)
        return pltpu.make_async_copy(pt.at[:, :, cols], PT.at[c, :, :, cols], pt_sem.at[i])

    def gate_up(slot, r):
        a = a_nat[r, :]
        g, u = dot(a, w_cols(slot, G_)), dot(a, w_cols(slot, U_))
        sig = jax.nn.sigmoid(g)
        silu = g * sig
        return silu, u * (sig + silu * (1.0 - sig)), (silu * u).astype(BF)

    def put_pt(p, i):
        pt[:, :, tile(i)] = p.T.reshape(nx, BW, TM)

    def fwd(c, carry):
        slot = lax.rem(c, 2)
        wait_weights(slot)

        def one(i, _):
            @pl.when(i == 0)
            def _0():
                gF(c + 1)
                gB(c + 3)

            @pl.when(i == 1)
            def _1():
                gA(c + 4)
                gC(c + 3)

            @pl.when(i == 2)
            def _2():
                gE(c + 2)

            @pl.when(i == 3)
            def _3():
                gD(c + 3)

            tau = TILES * c + i
            pl.when(tau >= 2)(lambda: st_out(tau - 2).wait())
            pl.when(c >= 1)(lambda: pt_out(c - 1, i).wait())
            r = tile(i)
            silu, slope, p = gate_up(slot, r)
            sb = lax.rem(tau, 2)
            stb[sb, 0] = silu
            stb[sb, 1] = slope
            put_pt(p, i)
            st_out(tau).start()
            pt_out(c, i).start()
            for h in range(2):
                acc[r, h * DH:(h + 1) * DH] += dot(p, wd_half(slot, h))
            return _

        return lax.fori_loop(0, TILES, one, carry)

    lax.fori_loop(0, C, fwd, 0)
    a0t_out.wait()
    for tau in (TILES * C - 2, TILES * C - 1):
        st_out(tau).wait()
    for i in range(TILES):
        pt_out(C - 1, i).wait()

    def h1_out(i, h):
        r = tile(i, TN)
        return pltpu.make_async_copy(dgu.at[h, r], H1.at[h, r], ld_sem.at[2])

    def norm1(i, _):
        r = tile(i, TN)
        h = (both(dyv, r).astype(F32) + acc[r, :].astype(BF).astype(F32)).astype(BF)
        for e in range(2):
            dgu[e, r, :] = h[:, e * DH:(e + 1) * DH]
            h1_out(i, e).start()
        for c_ in halves(dy_ref.at[0], dyv, r, ld_sem.at[0]):
            c_.start()
        put_a(h.astype(F32), i)
        acc[r, :] = jnp.zeros((TN, D), F32)
        return _

    lax.fori_loop(0, NT, norm1, 0)
    pltpu.make_async_copy(dgu, H1, ld_sem.at[2]).wait()
    pltpu.make_async_copy(dyv, dyv, ld_sem.at[0]).wait()

    def weights_grads(m, slot, after_p, after_keep):
        send_lane(D_, m)
        lagged(x2, m - 1)
        lagged(y2, m - 2)
        send_lane(G_, m)
        send_lane(U_, m)
        before_keep(m)
        keep_lane(D_, m)
        after_p()
        keep_lane(G_, m)
        keep_lane(U_, m)
        x1(m)
        after_keep()

        def one(i, _):
            pl.when((i == 1) & (m >= 1))(lambda: x3(m - 1))
            r = tile(i)
            for h in range(2):
                acc[r, h * DH:(h + 1) * DH] += (
                    dot(dgu[G_, r, :], w_half(slot, G_, h), 1, 1) + dot(dgu[U_, r, :], w_half(slot, U_, h), 1, 1))
            return _

        lax.fori_loop(0, TILES, one, 0)

    def d_p(slot, r):
        return dot(dyv[0, r, :], wd_half(slot, 0), 1, 1) + dot(dyv[1, r, :], wd_half(slot, 1), 1, 1)

    def put_d(r, dp, silu, slope):
        dgu[G_, r, :] = (dp * slope).astype(BF)
        dgu[U_, r, :] = (dp * silu).astype(BF)

    h1_in = [pltpu.make_async_copy(H1.at[h], a_nat.at[:, pl.ds(h * DH, DH)], ld_sem.at[0]) for h in range(2)]
    a0t_in = pltpu.make_async_copy(A0T, a_t, ld_sem.at[1])
    x_in = pltpu.make_async_copy(x_ref.at[0], a_nat, ld_sem.at[2])

    def bwd1(c, carry):
        n = C + c
        slot = lax.rem(n, 2)
        wait_weights(slot)

        def one(i, _):
            @pl.when(i == 0)
            def _0():
                gB(n + 3)

            @pl.when(i == 1)
            def _1():
                gA(n + 4)
                gC(n + 3)
                lagged(y3, c - 3)

            @pl.when(i == 2)
            def _2():
                gE(n + 2)

            @pl.when(i == 3)
            def _3():
                gD(n + 3)

            r = tile(i)
            silu, slope, p = gate_up(slot, r)
            put_pt(p, i)
            put_d(r, d_p(slot, r), silu, slope)
            return _

        lax.fori_loop(0, TILES, one, carry)
        gF(n + 1)
        last = c == C - 1

        @pl.when(last)
        def _():
            for c_ in h1_in:
                c_.start()

        weights_grads(c, slot, lambda: None, lambda: pl.when(last)(a0t_in.start))
        return carry

    lax.fori_loop(0, C, bwd1, 0)

    def st_in(tau):
        return pltpu.make_async_copy(ST.at[tau], stb.at[lax.rem(tau, 2)], st_sem.at[lax.rem(tau, 2)])

    def pt_in(c):
        return pltpu.make_async_copy(PT.at[c], pt, pt_sem.at[0])

    load_weights(0, 0)
    st_in(0).start()
    pt_in(0).start()
    pltpu.make_async_copy(a_nat, a_nat, ld_sem.at[0]).wait()

    def norm_back(h, d, through):
        scale = lax.rsqrt(jnp.mean(h * h, -1, keepdims=True) + 1e-6)
        along = jnp.sum(d * h, -1, keepdims=True) * (scale * scale * scale) * (1.0 / D)
        return (through + (d * scale - h * along)).astype(BF)

    def mid(i, _):
        r = tile(i, TN)
        out = norm_back(a_nat[r, :].astype(F32), acc[r, :], both(dyv, r).astype(F32))
        for e in range(2):
            dyv[e, r, :] = out[:, e * DH:(e + 1) * DH]
        acc[r, :] = jnp.zeros((TN, D), F32)
        return _

    lax.fori_loop(0, NT, mid, 0)
    x_in.start()
    a0t_in.wait()

    def bwd0(c, carry):
        m = C + c
        slot = lax.rem(c, 2)
        wait_weights(slot)
        pl.when(c < C - 1)(lambda: load_weights(c + 1, lax.rem(c + 1, 2)))

        def one(i, _):
            tau = TILES * c + i
            pl.when(i == 1)(lambda: y3(m - 3))
            st_in(tau).wait()
            pl.when(tau < TILES * C - 1)(lambda: st_in(tau + 1).start())
            sb = lax.rem(tau, 2)
            r = tile(i)
            put_d(r, d_p(slot, r), stb[sb, 0], stb[sb, 1])
            return _

        lax.fori_loop(0, TILES, one, carry)
        pt_in(c).wait()
        weights_grads(m, slot, lambda: pl.when(c < C - 1)(lambda: pt_in(c + 1).start()), lambda: None)
        return carry

    lax.fori_loop(0, C, bwd0, 0)

    x_in.wait()
    M = 2 * C
    x2(M - 1)
    y2(M - 2)

    def by_out(i):
        r = tile(i, TN)
        return pltpu.make_async_copy(a_nat.at[r], by_x.at[0, r], ld_sem.at[0])

    def last_norm(i, _):
        r = tile(i, TN)
        a_nat[r, :] = norm_back(a_nat[r, :].astype(F32), acc[r, :], both(dyv, r).astype(F32))
        by_out(i).start()
        return _

    lax.fori_loop(0, NT, last_norm, 0)
    x3(M - 1)
    y3(M - 3)
    y3(M - 2)
    y2(M - 1)
    y3(M - 1)
    pltpu.make_async_copy(a_nat, by_x.at[0], ld_sem.at[0]).wait()
    out_done(M - 1)
    for q in range(3):
        d_copy(q, M - 1).wait_send()
    for t in range(6):
        x_copy(t, M - 1).wait_send()
    arrived(od.at[:, :, pl.ds(0, DH)], od_recv)

    def sent(n, _):
        for t in range(16):
            out_copy(t, n).wait_send()
        return _

    lax.fori_loop(0, N, sent, 0)


def solution(mesh):
    nx, ny = mesh.shape["s"] // CORES, mesh.shape["r"]

    def step(x, dy, w_gate, w_up, w_down):
        layers, dr, ff = w_gate.shape
        _, T, D = x.shape
        C = ff // (nx * BW)
        N, CW, DH, HR = layers * C, nx * BW, D // 2, dr // 2
        TM, TN = T // TILES, T // (2 * TILES)

        k = lax.rem(lax.axis_index("s"), CORES)
        cols = lambda w: w.reshape(layers, dr, nx, C, BW).transpose(0, 3, 1, 2, 4).reshape(N, dr, CW)
        give = lax.dynamic_slice_in_dim(w_down, (1 - k) * DH, DH, 2)
        stay = lax.dynamic_slice_in_dim(w_down, k * DH, DH, 2)
        pairs = [(i, i + 1 - 2 * (i % CORES)) for i in range(mesh.shape["s"])]
        got = lax.ppermute(give, "s", pairs)
        lane = jnp.where(k == 0, jnp.concatenate([stay, got], 1), jnp.concatenate([got, stay], 1))
        own = jnp.stack([cols(w_gate), cols(w_up), lane.reshape(N, BW, DH)], 1)

        hbm = pl.BlockSpec(memory_space=pltpu.HBM)
        shape = jax.ShapeDtypeStruct
        outs = pl.pallas_call(
            functools.partial(kernel, (nx, ny, C, T, D)),
            out_shape=[
                shape((1, T, D), BF), shape((N, 2, dr, CW), BF), shape((layers, w_down.shape[1], D), BF),
                shape((N, 3, CORES * nx, dr, CW), BF), shape((TILES * C, 2, TM, CW), F32), shape((C, nx, BW, T), BF),
                shape((nx, CORES, dr, T), BF), shape((2, T, DH), BF),
            ],
            in_specs=[hbm] * 3,
            out_specs=[hbm] * 8,
            scratch_shapes=[
                pltpu.VMEM((T, D), BF), pltpu.VMEM((nx, CORES, dr, T), BF), pltpu.VMEM((2, T, DH), BF), pltpu.VMEM((T, D), F32),
                pltpu.VMEM((2, 3, CORES * nx, dr, CW), BF), pltpu.VMEM((2, T, CW), BF), pltpu.VMEM((nx, BW, T), BF),
                pltpu.VMEM((2, 2, TM, CW), F32),
                pltpu.VMEM((3, nx, dr, CW), BF), pltpu.VMEM((2, 3, nx, dr, CW), BF), pltpu.VMEM((2, 3, dr, CW), F32),
                pltpu.VMEM((3, HR, CW), F32), pltpu.VMEM((3, HR, CW), F32), pltpu.VMEM((3, dr, CW), BF),
                pltpu.VMEM((3, HR, CW), BF), pltpu.VMEM((3, HR, CW), BF), pltpu.VMEM((3, HR, CW), BF), pltpu.VMEM((3, HR, CW), BF),
                pltpu.VMEM((2, 3, HR, CW), BF), pltpu.VMEM((2, 3, HR, CW), BF),
                pltpu.VMEM((3, 3, dr, CW), BF), pltpu.VMEM((3, 3, dr, CW), BF), pltpu.VMEM((3, 3, dr, CW), BF),
                pltpu.VMEM((3, 3, dr, CW), BF), pltpu.VMEM((3, 3, dr, CW), BF), pltpu.VMEM((3, 3, dr, CW), BF),
                pltpu.VMEM((3, dr, CW), BF),
                pltpu.SemaphoreType.DMA((N, 16)), pltpu.SemaphoreType.DMA((N, 16)), pltpu.SemaphoreType.DMA((2,)),
                pltpu.SemaphoreType.DMA((2,)), pltpu.SemaphoreType.DMA((TILES,)), pltpu.SemaphoreType.DMA((3,)),
                pltpu.SemaphoreType.DMA((9,)), pltpu.SemaphoreType.DMA((2, 3)), pltpu.SemaphoreType.DMA((2, 2)),
                pltpu.SemaphoreType.DMA((3, 4)), pltpu.SemaphoreType.DMA((2, 3, 6)), pltpu.SemaphoreType.DMA((4,)),
                pltpu.SemaphoreType.DMA((2,)), pltpu.SemaphoreType.DMA,
            ],
            compiler_params=pltpu.CompilerParams(collective_id=0, has_side_effects=True, vmem_limit_bytes=67043328),
            name="stack",
        )(x, dy, own)
        by_x, og, od = outs[:3]
        back = lambda q: og[:, q].reshape(layers, C, dr, nx, BW).transpose(0, 2, 3, 1, 4).reshape(layers, dr, ff)
        return by_x, back(0), back(1), od

    states, cut = P(("rep", "r", "s"), None, None), P(None, "s", None)
    return jax.shard_map(
        step,
        mesh=mesh,
        in_specs=(states, states) + (cut,) * 3,
        out_specs=(states,) + (P("rep", "s", None),) * 3,
        check_vma=False,
    )
```

time: 810 us -> 477 us (0.59)
  matrix products: 448 us -> 0 us
  Pallas kernels: 0 us -> 420 us
  waiting for transfers between devices: 290 us -> 0.01 us
  local copies, waits for them, and re-layouts: 29.7 us -> 48.5 us
  other arithmetic: 19.7 us -> 5.09 us
  between operations: 14.5 us -> 0.71 us
    dot_general x17 -> x0, matrix products: 448 us -> none  [the longest x6 160 us: layer(): up = jnp.dot(a, w['w_up'], preferred_element_type=jnp.float32)]
    pallas_call x0 -> x1, Pallas kernels: none -> 420 us  [step(): pl.pallas_call(functools.partial(kernel, (nx, ny, C, T, D)), out_shape=[s...]
    all_gather x6 -> x0, waiting for transfers between devices: 118 us -> none  [fetched(): lax.all_gather(w[number], 's', axis=0, tiled=True)]
    reduce_scatter x6 -> x0, waiting for transfers between devices: 115 us -> none  [summed(): lax.psum_scatter(term, 's', scatter_dimension=0, tiled=True)]
    psum x1 -> x0, waiting for transfers between devices: 54.9 us -> none  [summed(): lax.psum(lax.psum_scatter(term, 's', scatter_dimension=0, tiled=True), 'r')]
    another operation x0 -> x6, local copies, waits for them, and re-layouts: none -> 16.3 us  [the longest x4 13 us: step(): og[:, q].reshape(layers, C, dr, nx, BW).transpose(0, 2, 3, 1, 4)]
    unnamed x31 -> x14, local copies, waits for them, and re-layouts: 22.5 us -> 18.8 us
  transfers between devices with their start and end apart: 13 -> 1, of which waited for: 10 -> 0; matrix products, arithmetic and copies ran while one was open for 46% -> 3% of each run, Pallas kernels for 0% -> 0%
where the time goes in v1:
time: 477 us; the launch traced here: 476 us
  Pallas kernels  420 us (88%)
  local copies, waits for them, and re-layouts  48.5 us (10%)
  other arithmetic  5.09 us (1%)
    pallas_call x1, Pallas kernels, step(): pl.pallas_call(functools.partial(kernel, (nx, ny, C, T, D)), out_shape=[s...  420 us
    unnamed x14, local copies, waits for them, and re-layouts  18.8 us
    another operation x4, local copies, waits for them, and re-layouts, step(): og[:, q].reshape(layers, C, dr, nx, BW).transpose(0, 2, 3, 1, 4)  13 us
  transfers between devices with their start and end apart: 1, of which 0 were waited for; matrix products, arithmetic and copies ran while one was open for 3% of the time, Pallas kernels for 0%

profile of v1, /device:TPU:97, one launch (start us, length us, event | category | flops | bytes accessed | tf_op | source)
XLA Modules:
  0.0 476.4 jit_solution(8910666491202481101)
XLA Ops:
  0.6 0.0 copy-start.2
  0.7 2.7 constant_dynamic-slice_fusion.1
  3.3 2.0 collective-permute-start
  5.4 0.0 copy-done.2
  5.4 2.2 copy.13
  7.6 3.5 copy.14
  11.2 1.6 stack_reshape.7
  12.8 3.8 copy.15
  16.6 3.5 copy.16
  20.2 1.6 stack_reshape.8
  21.8 0.0 collective-permute-done
  21.8 0.0 copy-start
  21.8 0.0 copy-start.1
  21.8 2.1 maximum_select_fusion
  24.0 0.0 copy-done
  24.0 0.4 copy-done.1
  24.4 2.9 pad_maximum_fusion.own
  27.4 420.1 %stack.5 = (bf16[1,2048,1024]{2,1,0:T(8,128)(2,1)}, bf16[14,2,128,512]{3,2,1,0:T(8,128)(2,1)}, bf16[2,448,1024]{2,1,0:T(8,128)(2,1)}, bf16[14,3,8,128,512]{4,3,2...) custom-call(bf16[1,2048,1024]{2,1,0:T(8,128)(2,1)} %x_ref.1, ...), custom_call_target="tpu_custom_call" | custom-call | tf_op jit(solution)/shard_map/stack/pallas_call | solution.py:644
  447.5 3.6 fusion
  451.1 4.2 reshape_squeeze.7
  455.3 4.2 copy.18
  459.4 3.8 copy.20
  463.3 1.4 reshape_squeeze.6
  464.7 3.3 copy.17
  468.0 2.4 copy.19
  470.4 0.0 copy-start.3
  470.4 4.8 %copy.23 = bf16[1,2048,1024]{2,1,0:T(8,128)(2,1)} copy(bf16[1,2048,1024]{2,1,0:T(8,128)(2,1)} %get-tuple-element.22) | data formatting | bytes 8388608
  475.2 0.0 copy-done.3
  475.2 1.2 copy.24
Async XLA Ops:
  0.6 4.7 copy-start.2
  3.3 18.5 %collective-permute-start = (bf16[2,448,512]{2,1,0:T(8,128)(2,1)}, bf16[2,448,512]{2,1,0:T(8,128)(2,1)}, u32[]{:S(2)}, u32[]{:S(2)}) collective-permute-start(bf16[2,448,512]{2,1,0:T(8,128)(2,1)} %get-tuple-element.17), channel_id=1, source_target_pairs={{0,1},{1,0},{2,3},{3,2},{4,5},{5,4},{6,7},{7,6},{8,9},{9,8},{10,11... | collective-permute-start | bytes 2752520 | tf_op jit(solution)/shard_map/ppermute | solution.py:638
  21.8 2.2 copy-start
  21.8 2.6 copy-start.1
  470.4 4.8 %copy-start.3 = (bf16[2,448,1024]{2,1,0:T(8,128)(2,1)S(1)}, bf16[2,448,1024]{2,1,0:T(8,128)(2,1)}, u32[]{:S(2)}) copy-start(bf16[2,448,1024]{2,1,0:T(8,128)(2,1)} %get-tuple-element.25) | copy-start | bytes 5505028

commit v2 on v1

--- a/solution.py
+++ b/solution.py
@@ -11,7 +11,8 @@
 MESH = pl.DeviceIdType.MESH
 CORES = 2
 BW = 128
-TILES = 4
+TILES = 2
+SUB = 4
 G_, U_, D_ = 0, 1, 2
 
 
@@ -27,11 +28,12 @@
         pl.when(condition)(f)
 
 
-def kernel(dims, x_ref, dy_ref, own,
-           by_x, og, od, G, ST, PT, A0T, H1,
-           a_nat, a_t, dyv, acc, wbuf, dgu, pt, stb,
+def kernel(dims, x_ref, dy_ref, wg_ref, wu_ref, wd_ref,
+           by_x, og, ou, od, G, WDO, ST, PT, A0T, H1,
+           a_nat, a_t, dyv, acc, wbuf, dgu, pt, stb, own_v,
            s_send, d_recv, own32, r32, l32, s_u1, s_pr, s_pl, u2r, u2l, ra, rb, rc, rd, v, ya, yb, yc, f_out,
-           g_send, g_recv, w_sem, st_sem, pt_sem, ld_sem, rs_send, d_sem, x_sem, rc_sem, y_sem, o_sem, od_send, od_recv):
+           g_send, g_recv, w_sem, st_sem, pt_sem, ld_sem, rs_send, d_sem, x_sem, rc_sem, y_sem, o_sem, od_send, od_recv,
+           own_sem, own_out, ex_send, ex_recv):
     nx, ny, C, T, D = dims
     TM = T // TILES
     N = 2 * C
@@ -76,7 +78,7 @@
             12: (None, full, sib), 13: (pL, full, sib), 14: (pR, full, sib), 15: (pO, full, sib),
         }
         j, r, who = spec[t]
-        src = own.at[n, :, r, :] if j is None else G.at[n, :, j, r, :]
+        src = own_v.at[lax.rem(n, 4), :, r, :] if j is None else G.at[n, :, j, r, :]
         return remote(src, G.at[n, :, s if j is None else j, r, :], g_send.at[n, t], g_recv.at[n, t], who)
 
     def in_wait(t, n):
@@ -92,18 +94,78 @@
         j, r = spec[t]
         arrived(G.at[n, :, j, r, :], g_recv.at[n, t])
 
+    def named(f):
+        def run(*args):
+            with jax.named_scope(f.__name__):
+                return f(*args)
+        return run
+
     def stage(f):
-        def run(n):
-            when((n >= 0) & (n < N) if not isinstance(n, int) else 0 <= n < N, lambda: f(n))
-        return run
+        return lambda n: when((n >= 0) & (n < N) if not isinstance(n, int) else 0 <= n < N, lambda: named(f)(n))
 
     def starts(n, *ts):
         for t in ts:
             out_copy(t, n).start()
 
+    def layer_of(n):
+        if isinstance(n, int):
+            return n // C, n % C
+        second = n >= C
+        return jnp.where(second, 1, 0), jnp.where(second, n - C, n)
+
+    def block_cols(j, c):
+        return pl.ds(pl.multiple_of((j * C + c) * BW, BW), BW)
+
+    def half_block(h):
+        o = jnp.where(h >= C, 1, 0)
+        return o, pl.ds(pl.multiple_of(HR * (h - C * o), HR), HR)
+
+    def core_cols(core):
+        return pl.ds(pl.multiple_of(core * DH, DH), DH)
+
+    def exchange(layer):
+        mine_ = pl.ds(pl.multiple_of(k * C * HR, HR), C * HR)
+        return remote(wd_ref.at[layer, :, core_cols(1 - k)], WDO.at[layer, mine_], ex_send.at[layer], ex_recv.at[layer], sib)
+
+    def exchanged(layer):
+        theirs = pl.ds(pl.multiple_of((1 - k) * C * HR, HR), C * HR)
+        arrived(WDO.at[layer, theirs], ex_recv.at[layer])
+
+    def free_own(n):
+        for t in (0, 1, 2, 3, 12):
+            out_copy(t, n).wait_send()
+
+    def own_down(n):
+        slot, (layer, c) = lax.rem(n, 4), layer_of(n)
+        for e in range(2):
+            h = 2 * c + e
+            o, r = half_block(h)
+            dst, sem = own_v.at[slot, D_, pl.ds(e * HR, HR)], own_sem.at[slot]
+            far = pl.ds(pl.multiple_of(HR * h, HR), HR)
+            pl.when(o == k)(lambda: pltpu.make_async_copy(wd_ref.at[layer, r, core_cols(k)], dst, sem).start())
+            pl.when(o != k)(lambda: pltpu.make_async_copy(WDO.at[layer, far], dst, sem).start())
+
+    def own_cols(n):
+        slot, (layer, c) = lax.rem(n, 4), layer_of(n)
+        for q, w in ((G_, wg_ref), (U_, wu_ref)):
+            for j in range(nx):
+                pltpu.make_async_copy(w.at[layer, :, block_cols(j, c)], own_v.at[slot, q, :, pl.ds(j * BW, BW)], own_sem.at[slot]).start()
+
+    @stage
+    def gS(n):
+        when(n >= 4, lambda: free_own(n - 4))
+        own_cols(n)
+        own_down(n)
+
+    def own_stored(n):
+        return pltpu.make_async_copy(own_v.at[lax.rem(n, 4)], G.at[n, :, s], own_out.at[lax.rem(n, 4)])
+
     @stage
     def gA(n):
+        slot = lax.rem(n, 4)
+        pltpu.make_async_copy(own_v.at[slot], own_v.at[slot], own_sem.at[slot]).wait()
         starts(n, 0, 2, 1, 3, 12)
+        own_stored(n).start()
 
     @stage
     def gB(n):
@@ -132,13 +194,13 @@
             in_wait(a, n)
             in_wait(b, n)
             starts(n, t)
+        own_stored(n).wait()
 
     def load_weights(n, slot):
-        pltpu.make_async_copy(own.at[n], wbuf.at[slot, :, s], w_sem.at[slot]).start()
-        for j in range(1, CORES * nx):
-            p = lax.rem(s + j, CORES * nx)
+        for p in range(CORES * nx):
             pltpu.make_async_copy(G.at[n, :, p], wbuf.at[slot, :, p], w_sem.at[slot]).start()
 
+    @named
     def wait_weights(slot):
         pltpu.make_async_copy(wbuf.at[slot], wbuf.at[slot], w_sem.at[slot]).wait()
 
@@ -177,9 +239,26 @@
         return remote(s_send.at[q], d_recv.at[lax.rem(m, 2), q], rs_send.at[q], d_sem.at[lax.rem(m, 2), q], sib)
 
     def send_lane(q, m):
-        when(m > 0, lambda: d_copy(q, m).wait_send())
         s_send[q] = grad(q, 1 - k).astype(BF).reshape(nx, DR, CW)
-        d_copy(q, m).start()
+
+    @named
+    def send_lanes(m):
+        def f():
+            for q in (D_, G_, U_):
+                d_copy(q, m - 1).wait_send()
+        when(m > 0, f)
+        when(m >= 3, lambda: y3_wait(m - 3))
+        send_lane(D_, m)
+        y3_add(m - 3)
+        send_lane(G_, m)
+        d_copy(D_, m).start()
+        d_copy(G_, m).start()
+        when(m >= 3, lambda: y3_out(m - 3))
+        when(m >= 1, lambda: x2_wait(m - 1))
+        send_lane(U_, m)
+        x2_add(m - 1)
+        d_copy(U_, m).start()
+        when(m >= 1, lambda: x2_out(m - 1))
 
     lo, hi = pl.ds(0, HR), pl.ds(HR, HR)
 
@@ -225,28 +304,35 @@
                4: yc.at[three, :, lo], 5: yc.at[three, :, hi]}[t]
         arrived(dst, y_sem.at[1, three, t])
 
-    def keep_lane(q, m):
+    @named
+    def keep_lanes(m):
         two = lax.rem(m, 2)
-        arrived(d_recv.at[two, q], d_sem.at[two, q])
-        total = (grad(q, k) + d_recv[two, q].reshape(CW, CW).astype(F32)).reshape(nx, DR, CW)
-        own32[two, q] = total[0]
-        r32[q] = total[1, :HR]
-        s_pr[q] = total[1, HR:].astype(BF)
-        s_u1[q] = total[2].astype(BF)
-        s_pl[q] = total[3, :HR].astype(BF)
-        l32[q] = total[3, HR:]
-
-    def before_keep(m):
+
         def f():
             for t in range(4):
                 x_copy(t, m - 1).wait_send()
         when(m > 0, f)
-
+        for q in (D_, G_, U_):
+            arrived(d_recv.at[two, q], d_sem.at[two, q])
+        for q in (D_, G_, U_):
+            total = (grad(q, k) + d_recv[two, q].reshape(CW, CW).astype(F32)).reshape(nx, DR, CW)
+            own32[two, q] = total[0]
+            r32[q] = total[1, :HR]
+            s_pr[q] = total[1, HR:].astype(BF)
+            s_u1[q] = total[2].astype(BF)
+            s_pl[q] = total[3, :HR].astype(BF)
+            l32[q] = total[3, HR:]
+
+    @named
     def x1(m):
         for t in range(4):
             x_copy(t, m).start()
 
-    def x2(m):
+    def slot_of(m, n):
+        return lax.rem(m + n, n)
+
+    @named
+    def x2_wait(m):
         x_wait(0, m)
         x_wait(1, m)
 
@@ -254,13 +340,23 @@
             x_copy(4, m - 1).wait_send()
             x_copy(5, m - 1).wait_send()
         when(m > 0, f)
-        two = lax.rem(m, 2)
+
+    def x2_add(m):
+        two = slot_of(m, 2)
         for q in range(3):
             u2r[q] = (r32[q] + ra[two, q].astype(F32)).astype(BF)
             u2l[q] = (l32[q] + rb[two, q].astype(F32)).astype(BF)
+
+    def x2_out(m):
         x_copy(4, m).start()
         x_copy(5, m).start()
 
+    def x2(m):
+        x2_wait(m)
+        x2_add(m)
+        x2_out(m)
+
+    @named
     def x3(m):
         for t in (2, 3, 4, 5):
             x_wait(t, m)
@@ -270,6 +366,7 @@
         for t in range(4):
             y_copy(t, m).start()
 
+    @named
     def y2(m):
         y_wait(0, m)
         y_copy(4, m).start()
@@ -280,44 +377,51 @@
         first = m < C
         return jnp.where(first, 1, 0), jnp.where(first, m, m - C)
 
-    def od_place(h):
-        o = jnp.where(h >= C, 1, 0)
-        return o, pl.ds(pl.multiple_of(HR * (h - C * o), HR), HR)
-
-    def od_cols():
-        return pl.ds(pl.multiple_of(k * DH, DH), DH)
-
-    def og_copy(q, m):
+    def cols_out(q, m):
         layer, c = where_m(m)
-        return pltpu.make_async_copy(f_out.at[q], og.at[layer * C + c, q], o_sem.at[q])
+        return [pltpu.make_async_copy(f_out.at[q, :, pl.ds(j * BW, BW)], (og, ou)[q].at[layer, :, block_cols(j, c)], o_sem.at[q])
+                for j in range(nx)]
 
     def od_each(m, local, far):
         layer, c = where_m(m)
         for e in range(2):
-            o, r = od_place(2 * c + e)
-            src, dst = f_out.at[D_, pl.ds(e * HR, HR)], od.at[layer, r, od_cols()]
+            o, r = half_block(2 * c + e)
+            src, dst = f_out.at[D_, pl.ds(e * HR, HR)], od.at[layer, r, core_cols(k)]
             pl.when(o == k)(functools.partial(local, pltpu.make_async_copy(src, dst, o_sem.at[2 + e])))
             pl.when(o != k)(functools.partial(far, remote(src, dst, od_send.at[e], od_recv, sib)))
 
+    @named
     def out_done(m):
         for q in (G_, U_):
-            og_copy(q, m).wait()
+            pltpu.make_async_copy(f_out.at[q], f_out.at[q], o_sem.at[q]).wait()
         od_each(m, lambda c: c.wait(), lambda c: c.wait_send())
 
-    def y3(m):
+    @named
+    def y3_wait(m):
         for t in (1, 3, 4, 5):
             y_wait(t, m)
         when(m > 0, lambda: out_done(m - 1))
-        three = lax.rem(m, 3)
+
+    def y3_add(m):
+        three = slot_of(m, 3)
         for q in range(3):
             a = v[three, q].astype(F32) + yc[three, q].astype(F32)
             b = ya[three, q].astype(F32) + yb[three, q].astype(F32)
             f_out[q] = (a + b).astype(BF)
+
+    @named
+    def y3_out(m):
         for t in range(6):
             y_copy(t, m).wait_send()
         for q in (G_, U_):
-            og_copy(q, m).start()
+            for c_ in cols_out(q, m):
+                c_.start()
         od_each(m, lambda c: c.start(), lambda c: c.start())
+
+    def y3(m):
+        y3_wait(m)
+        y3_add(m)
+        y3_out(m)
 
     def lagged(f, m):
         when(m >= 0, lambda: f(m))
@@ -326,12 +430,18 @@
         return [pltpu.make_async_copy(src.at[r, pl.ds(h * DH, DH)], dst.at[h, r], sem) for h in range(2)]
 
     every = pl.ds(0, T)
+    for layer in range(2):
+        exchange(layer).start()
+    own_cols(0)
     for c_ in halves(x_ref.at[0], dyv, every, ld_sem.at[0]):
         c_.start()
+    exchanged(0)
+    own_down(0)
     gA(0)
+    gS(1)
     pltpu.make_async_copy(dyv, dyv, ld_sem.at[0]).wait()
 
-    NT = 2 * TILES
+    NT = 4 * TILES
     TN = T // NT
 
     def both(ref, r):
@@ -353,24 +463,24 @@
     lax.fori_loop(0, NT, norm0, 0)
     a0t_out = pltpu.make_async_copy(a_t, A0T, ld_sem.at[1])
     a0t_out.start()
+    exchanged(1)
     gB(0)
     gA(1)
+    gS(2)
     gC(0)
     gD(0)
     gB(1)
     gA(2)
+    gS(3)
     gC(1)
     gE(0)
+    gF(0)
     gD(1)
-    gF(0)
     gB(2)
-    gA(3)
-    gC(2)
-    gE(1)
-    gD(2)
 
     def st_out(tau):
-        return pltpu.make_async_copy(stb.at[lax.rem(tau, 2)], ST.at[tau], st_sem.at[lax.rem(tau, 2)])
+        i = lax.rem(tau, TILES)
+        return pltpu.make_async_copy(stb.at[i], ST.at[tau], st_sem.at[i])
 
     def pt_out(c, i):
         cols = tile(i)
@@ -384,7 +494,7 @@
         return silu, u * (sig + silu * (1.0 - sig)), (silu * u).astype(BF)
 
     def put_pt(p, i):
-        pt[:, :, tile(i)] = p.T.reshape(nx, BW, TM)
+        pt[:, :, tile(i, TM // SUB)] = p.T.reshape(nx, BW, TM // SUB)
 
     def fwd(c, carry):
         slot = lax.rem(c, 2)
@@ -393,44 +503,48 @@
         def one(i, _):
             @pl.when(i == 0)
             def _0():
-                gF(c + 1)
-                gB(c + 3)
+                gA(c + 3)
+                gS(c + 4)
+                pl.when(c > 0)(lambda: gE(c + 1))
 
             @pl.when(i == 1)
             def _1():
-                gA(c + 4)
-                gC(c + 3)
-
-            @pl.when(i == 2)
+                gC(c + 2)
+                gD(c + 2)
+                pl.when(c == 0)(lambda: gE(c + 1))
+
+            tau = TILES * c + i
+            @pl.when(c >= 1)
             def _2():
-                gE(c + 2)
-
-            @pl.when(i == 3)
-            def _3():
-                gD(c + 3)
-
-            tau = TILES * c + i
-            pl.when(tau >= 2)(lambda: st_out(tau - 2).wait())
-            pl.when(c >= 1)(lambda: pt_out(c - 1, i).wait())
-            r = tile(i)
-            silu, slope, p = gate_up(slot, r)
-            sb = lax.rem(tau, 2)
-            stb[sb, 0] = silu
-            stb[sb, 1] = slope
-            put_pt(p, i)
-            st_out(tau).start()
-            pt_out(c, i).start()
+                st_out(tau - TILES).wait()
+                pt_out(c - 1, i).wait()
+
+            with jax.named_scope("fwd_up"):
+                for j in range(SUB):
+                    e = SUB * i + j
+                    r = tile(e, TM // SUB)
+                    silu, slope, p = gate_up(slot, r)
+                    inner = pl.ds(j * (TM // SUB), TM // SUB)
+                    stb[i, 0, inner] = silu
+                    stb[i, 1, inner] = slope
+                    put_pt(p, e)
+                    dgu[0, r, :] = p
+                st_out(tau).start()
+                pt_out(c, i).start()
+            return _
+
+        lax.fori_loop(0, TILES, one, carry)
+        gB(c + 3)
+        gF(c + 1)
+        with jax.named_scope("fwd_down"):
             for h in range(2):
-                acc[r, h * DH:(h + 1) * DH] += dot(p, wd_half(slot, h))
-            return _
-
-        return lax.fori_loop(0, TILES, one, carry)
+                acc[:, h * DH:(h + 1) * DH] += dot(dgu[0], wd_half(slot, h))
+        return carry
 
     lax.fori_loop(0, C, fwd, 0)
     a0t_out.wait()
-    for tau in (TILES * C - 2, TILES * C - 1):
-        st_out(tau).wait()
     for i in range(TILES):
+        st_out(TILES * (C - 1) + i).wait()
         pt_out(C - 1, i).wait()
 
     def h1_out(i, h):
@@ -453,30 +567,6 @@
     pltpu.make_async_copy(dgu, H1, ld_sem.at[2]).wait()
     pltpu.make_async_copy(dyv, dyv, ld_sem.at[0]).wait()
 
-    def weights_grads(m, slot, after_p, after_keep):
-        send_lane(D_, m)
-        lagged(x2, m - 1)
-        lagged(y2, m - 2)
-        send_lane(G_, m)
-        send_lane(U_, m)
-        before_keep(m)
-        keep_lane(D_, m)
-        after_p()
-        keep_lane(G_, m)
-        keep_lane(U_, m)
-        x1(m)
-        after_keep()
-
-        def one(i, _):
-            pl.when((i == 1) & (m >= 1))(lambda: x3(m - 1))
-            r = tile(i)
-            for h in range(2):
-                acc[r, h * DH:(h + 1) * DH] += (
-                    dot(dgu[G_, r, :], w_half(slot, G_, h), 1, 1) + dot(dgu[U_, r, :], w_half(slot, U_, h), 1, 1))
-            return _
-
-        lax.fori_loop(0, TILES, one, 0)
-
     def d_p(slot, r):
         return dot(dyv[0, r, :], wd_half(slot, 0), 1, 1) + dot(dyv[1, r, :], wd_half(slot, 1), 1, 1)
 
@@ -488,100 +578,139 @@
     a0t_in = pltpu.make_async_copy(A0T, a_t, ld_sem.at[1])
     x_in = pltpu.make_async_copy(x_ref.at[0], a_nat, ld_sem.at[2])
 
-    def bwd1(c, carry):
-        n = C + c
-        slot = lax.rem(n, 2)
+    def st_load(c):
+        for i in range(TILES):
+            for e in range(2):
+                pltpu.make_async_copy(ST.at[TILES * c + i, e], stb.at[i, e], st_sem.at[i]).start()
+
+    def st_wait(i):
+        pltpu.make_async_copy(stb.at[i], stb.at[i], st_sem.at[i]).wait()
+
+    def pt_in(c):
+        return pltpu.make_async_copy(PT.at[c], pt, pt_sem.at[0])
+
+    def norm_back(h, d, through):
+        scale = lax.rsqrt(jnp.mean(h * h, -1, keepdims=True) + 1e-6)
+        along = jnp.sum(d * h, -1, keepdims=True) * (scale * scale * scale) * (1.0 / D)
+        return (through + (d * scale - h * along)).astype(BF)
+
+    def middle():
+        pltpu.make_async_copy(a_nat, a_nat, ld_sem.at[0]).wait()
+
+        def mid(i, _):
+            with jax.named_scope("mid"):
+                r = tile(i, TN)
+                out = norm_back(a_nat[r, :].astype(F32), acc[r, :], both(dyv, r).astype(F32))
+                for e in range(2):
+                    dyv[e, r, :] = out[:, e * DH:(e + 1) * DH]
+                acc[r, :] = jnp.zeros((TN, D), F32)
+            return _
+
+        lax.fori_loop(0, NT, mid, 0)
+        x_in.start()
+        a0t_in.wait()
+
+    at_hook = {
+        0: {0: [(gA, 3), (gE, 1), (gS, 4)], 1: [(gS, 6)]},
+        1: {0: [(gC, 2), (gD, 2), (gB, 3), (gA, 4), (gS, 5)], 1: [(gC, 5), (gA, 6)], 2: [(gD, 6), (gE, 5)], 3: [(gE, 6)]},
+        2: {},
+        3: {0: [(gE, 2), (gC, 3), (gD, 3), (gB, 4), (gA, 5)], 1: [(gB, 6), (gC, 6)]},
+        4: {0: [(gC, 4)], 1: [(gD, 5)]},
+        5: {0: [(gD, 4), (gE, 3), (gB, 5)], 1: [(gE, 4)]},
+    }
+
+    def hook(h, m):
+        for step, todo in at_hook[h].items():
+            @pl.when(m == step)
+            def _(todo=todo):
+                for f, n in todo:
+                    f(C + n)
+
+    def bwd(m, carry):
+        slot = lax.rem(m + 1, 2)
+        last = m == C - 1
+        first_layer = m >= C
+        pl.when(m == C)(middle)
         wait_weights(slot)
 
-        def one(i, _):
-            @pl.when(i == 0)
-            def _0():
-                gB(n + 3)
-
-            @pl.when(i == 1)
-            def _1():
-                gA(n + 4)
-                gC(n + 3)
-                lagged(y3, c - 3)
-
-            @pl.when(i == 2)
-            def _2():
-                gE(n + 2)
-
-            @pl.when(i == 3)
-            def _3():
-                gD(n + 3)
-
-            r = tile(i)
-            silu, slope, p = gate_up(slot, r)
-            put_pt(p, i)
-            put_d(r, d_p(slot, r), silu, slope)
-            return _
-
-        lax.fori_loop(0, TILES, one, carry)
-        gF(n + 1)
-        last = c == C - 1
+        @pl.when(first_layer & (m < 2 * C - 1))
+        def _():
+            load_weights(m + 1 - C, 1 - slot)
+
+        hook(0, m)
+
+        @pl.when(jnp.logical_not(first_layer))
+        def _():
+            def one(i, _):
+                @pl.when(i == 1)
+                def _1():
+                    hook(1, m)
+
+                with jax.named_scope("bwd1_tile"):
+                    for j in range(SUB):
+                        e = SUB * i + j
+                        r = tile(e, TM // SUB)
+                        silu, slope, p = gate_up(slot, r)
+                        put_pt(p, e)
+                        put_d(r, d_p(slot, r), silu, slope)
+                return _
+
+            lax.fori_loop(0, TILES, one, 0)
+
+        @pl.when(first_layer)
+        def _():
+            def one(i, _):
+                st_wait(i)
+                with jax.named_scope("bwd0_tile"):
+                    r = tile(i)
+                    put_d(r, d_p(slot, r), stb[i, 0], stb[i, 1])
+                return _
+
+            lax.fori_loop(0, TILES, one, 0)
+            pt_in(m - C).wait()
+
+        hook(2, m)
 
         @pl.when(last)
         def _():
             for c_ in h1_in:
                 c_.start()
-
-        weights_grads(c, slot, lambda: None, lambda: pl.when(last)(a0t_in.start))
+            load_weights(0, 1 - slot)
+
+        @pl.when((m >= C - 1) & (m < 2 * C - 1))
+        def _():
+            st_load(m + 1 - C)
+
+        send_lanes(m)
+        lagged(y2, m - 2)
+        hook(3, m)
+        pl.when(m < C - 1)(lambda: gF(C + 1 + m))
+
+        def d_a(i):
+            with jax.named_scope("da_tile"):
+                r = tile(i)
+                for h in range(2):
+                    acc[r, h * DH:(h + 1) * DH] += (
+                        dot(dgu[G_, r, :], w_half(slot, G_, h), 1, 1) + dot(dgu[U_, r, :], w_half(slot, U_, h), 1, 1))
+
+        def rest(i, _):
+            d_a(i)
+
+            @pl.when(i == 0)
+            def _0():
+                hook(4, m)
+                keep_lanes(m)
+                x1(m)
+                hook(5, m)
+                pl.when((m >= C - 1) & (m < 2 * C - 1))(lambda: pt_in(m + 1 - C).start())
+                pl.when(last)(a0t_in.start)
+            return _
+
+        lax.fori_loop(0, TILES, rest, 0)
+        lagged(x3, m - 1)
         return carry
 
-    lax.fori_loop(0, C, bwd1, 0)
-
-    def st_in(tau):
-        return pltpu.make_async_copy(ST.at[tau], stb.at[lax.rem(tau, 2)], st_sem.at[lax.rem(tau, 2)])
-
-    def pt_in(c):
-        return pltpu.make_async_copy(PT.at[c], pt, pt_sem.at[0])
-
-    load_weights(0, 0)
-    st_in(0).start()
-    pt_in(0).start()
-    pltpu.make_async_copy(a_nat, a_nat, ld_sem.at[0]).wait()
-
-    def norm_back(h, d, through):
-        scale = lax.rsqrt(jnp.mean(h * h, -1, keepdims=True) + 1e-6)
-        along = jnp.sum(d * h, -1, keepdims=True) * (scale * scale * scale) * (1.0 / D)
-        return (through + (d * scale - h * along)).astype(BF)
-
-    def mid(i, _):
-        r = tile(i, TN)
-        out = norm_back(a_nat[r, :].astype(F32), acc[r, :], both(dyv, r).astype(F32))
-        for e in range(2):
-            dyv[e, r, :] = out[:, e * DH:(e + 1) * DH]
-        acc[r, :] = jnp.zeros((TN, D), F32)
-        return _
-
-    lax.fori_loop(0, NT, mid, 0)
-    x_in.start()
-    a0t_in.wait()
-
-    def bwd0(c, carry):
-        m = C + c
-        slot = lax.rem(c, 2)
-        wait_weights(slot)
-        pl.when(c < C - 1)(lambda: load_weights(c + 1, lax.rem(c + 1, 2)))
-
-        def one(i, _):
-            tau = TILES * c + i
-            pl.when(i == 1)(lambda: y3(m - 3))
-            st_in(tau).wait()
-            pl.when(tau < TILES * C - 1)(lambda: st_in(tau + 1).start())
-            sb = lax.rem(tau, 2)
-            r = tile(i)
-            put_d(r, d_p(slot, r), stb[sb, 0], stb[sb, 1])
-            return _
-
-        lax.fori_loop(0, TILES, one, carry)
-        pt_in(c).wait()
-        weights_grads(m, slot, lambda: pl.when(c < C - 1)(lambda: pt_in(c + 1).start()), lambda: None)
-        return carry
-
-    lax.fori_loop(0, C, bwd0, 0)
+    lax.fori_loop(0, 2 * C, bwd, 0)
 
     x_in.wait()
     M = 2 * C
@@ -611,10 +740,13 @@
     for t in range(6):
         x_copy(t, M - 1).wait_send()
     arrived(od.at[:, :, pl.ds(0, DH)], od_recv)
+    for layer in range(2):
+        exchange(layer).wait_send()
 
     def sent(n, _):
-        for t in range(16):
+        for t in (4, 5, 6, 7, 8, 9, 10, 11, 13, 14, 15):
             out_copy(t, n).wait_send()
+        pl.when(n >= N - 4)(lambda: free_own(n))
         return _
 
     lax.fori_loop(0, N, sent, 0)
@@ -628,32 +760,24 @@
         _, T, D = x.shape
         C = ff // (nx * BW)
         N, CW, DH, HR = layers * C, nx * BW, D // 2, dr // 2
-        TM, TN = T // TILES, T // (2 * TILES)
-
-        k = lax.rem(lax.axis_index("s"), CORES)
-        cols = lambda w: w.reshape(layers, dr, nx, C, BW).transpose(0, 3, 1, 2, 4).reshape(N, dr, CW)
-        give = lax.dynamic_slice_in_dim(w_down, (1 - k) * DH, DH, 2)
-        stay = lax.dynamic_slice_in_dim(w_down, k * DH, DH, 2)
-        pairs = [(i, i + 1 - 2 * (i % CORES)) for i in range(mesh.shape["s"])]
-        got = lax.ppermute(give, "s", pairs)
-        lane = jnp.where(k == 0, jnp.concatenate([stay, got], 1), jnp.concatenate([got, stay], 1))
-        own = jnp.stack([cols(w_gate), cols(w_up), lane.reshape(N, BW, DH)], 1)
+        TM = T // TILES
 
         hbm = pl.BlockSpec(memory_space=pltpu.HBM)
         shape = jax.ShapeDtypeStruct
         outs = pl.pallas_call(
             functools.partial(kernel, (nx, ny, C, T, D)),
             out_shape=[
-                shape((1, T, D), BF), shape((N, 2, dr, CW), BF), shape((layers, w_down.shape[1], D), BF),
-                shape((N, 3, CORES * nx, dr, CW), BF), shape((TILES * C, 2, TM, CW), F32), shape((C, nx, BW, T), BF),
+                shape((1, T, D), BF), shape(w_gate.shape, BF), shape(w_up.shape, BF), shape(w_down.shape, BF),
+                shape((N, 3, CORES * nx, dr, CW), BF), shape((layers, C * BW, DH), BF),
+                shape((TILES * C, 2, TM, CW), F32), shape((C, nx, BW, T), BF),
                 shape((nx, CORES, dr, T), BF), shape((2, T, DH), BF),
             ],
-            in_specs=[hbm] * 3,
-            out_specs=[hbm] * 8,
+            in_specs=[hbm] * 5,
+            out_specs=[hbm] * 10,
             scratch_shapes=[
                 pltpu.VMEM((T, D), BF), pltpu.VMEM((nx, CORES, dr, T), BF), pltpu.VMEM((2, T, DH), BF), pltpu.VMEM((T, D), F32),
                 pltpu.VMEM((2, 3, CORES * nx, dr, CW), BF), pltpu.VMEM((2, T, CW), BF), pltpu.VMEM((nx, BW, T), BF),
-                pltpu.VMEM((2, 2, TM, CW), F32),
+                pltpu.VMEM((TILES, 2, TM, CW), F32), pltpu.VMEM((4, 3, dr, CW), BF),
                 pltpu.VMEM((3, nx, dr, CW), BF), pltpu.VMEM((2, 3, nx, dr, CW), BF), pltpu.VMEM((2, 3, dr, CW), F32),
                 pltpu.VMEM((3, HR, CW), F32), pltpu.VMEM((3, HR, CW), F32), pltpu.VMEM((3, dr, CW), BF),
                 pltpu.VMEM((3, HR, CW), BF), pltpu.VMEM((3, HR, CW), BF), pltpu.VMEM((3, HR, CW), BF), pltpu.VMEM((3, HR, CW), BF),
@@ -666,13 +790,12 @@
                 pltpu.SemaphoreType.DMA((9,)), pltpu.SemaphoreType.DMA((2, 3)), pltpu.SemaphoreType.DMA((2, 2)),
                 pltpu.SemaphoreType.DMA((3, 4)), pltpu.SemaphoreType.DMA((2, 3, 6)), pltpu.SemaphoreType.DMA((4,)),
                 pltpu.SemaphoreType.DMA((2,)), pltpu.SemaphoreType.DMA,
+                pltpu.SemaphoreType.DMA((4,)), pltpu.SemaphoreType.DMA((4,)), pltpu.SemaphoreType.DMA((2,)), pltpu.SemaphoreType.DMA((2,)),
             ],
             compiler_params=pltpu.CompilerParams(collective_id=0, has_side_effects=True, vmem_limit_bytes=67043328),
             name="stack",
-        )(x, dy, own)
-        by_x, og, od = outs[:3]
-        back = lambda q: og[:, q].reshape(layers, C, dr, nx, BW).transpose(0, 2, 3, 1, 4).reshape(layers, dr, ff)
-        return by_x, back(0), back(1), od
+        )(x, dy, w_gate, w_up, w_down)
+        return tuple(outs[:4])
 
     states, cut = P(("rep", "r", "s"), None, None), P(None, "s", None)
     return jax.shard_map(

time: 477 us -> 402 us (0.84)
  local copies, waits for them, and re-layouts: 48.5 us -> 10.3 us
  Pallas kernels: 420 us -> 391 us
  other arithmetic: 5.09 us -> 0 us
    pallas_call x1, Pallas kernels: 420 us -> 391 us  [step(): pl.pallas_call(functools.partial(kernel, (nx, ny, C, T, D)), out_shape=[s...]
    another operation x6 -> x0, local copies, waits for them, and re-layouts: 16.3 us -> none  [the longest x4 13 us: step(): og[:, q].reshape(layers, C, dr, nx, BW).transpose(0, 2, 3, 1, 4)]
    unnamed x14 -> x10, local copies, waits for them, and re-layouts: 18.8 us -> 10.3 us
    transpose x2 -> x0, local copies, waits for them, and re-layouts: 7.07 us -> none  [step(): w.reshape(layers, dr, nx, C, BW).transpose(0, 3, 1, 2, 4).reshape(N, dr, CW)]
  transfers between devices with their start and end apart: 1 -> 0, of which waited for: 0 -> 0; matrix products, arithmetic and copies ran while one was open for 3% -> 0% of each run, Pallas kernels for 0% -> 0%
where the time goes in v2:
time: 402 us
  Pallas kernels  391 us (97%)
  local copies, waits for them, and re-layouts  10.3 us (3%)
    pallas_call x1, Pallas kernels, step(): pl.pallas_call(functools.partial(kernel, (nx, ny, C, T, D)), out_shape=[s...  391 us
    unnamed x10, local copies, waits for them, and re-layouts  10.3 us

profile of v2, /device:TPU:97, one launch (start us, length us, event | category | flops | bytes accessed | tf_op | source)
XLA Modules:
  0.0 401.8 jit_solution(1983727342937441120)
XLA Ops:
  0.6 390.9 %stack.1 = (bf16[1,2048,1024]{2,1,0:T(8,128)(2,1)}, bf16[2,128,3584]{2,1,0:T(8,128)(2,1)}, bf16[2,128,3584]{2,1,0:T(8,128)(2,1)}, bf16[2,448,1024]{2,1,0:T(8,128...) custom-call(bf16[1,2048,1024]{2,1,0:T(8,128)(2,1)} %x_ref.1, ...), custom_call_target="tpu_custom_call" | custom-call | tf_op jit(solution)/shard_map/stack/pallas_call | solution.py:767
  391.5 0.0 copy-start.2
  391.5 4.8 %copy.13 = bf16[1,2048,1024]{2,1,0:T(8,128)(2,1)} copy(bf16[1,2048,1024]{2,1,0:T(8,128)(2,1)} %get-tuple-element.16) | data formatting | bytes 8388608
  396.3 0.0 copy-done.2
  396.3 0.0 copy-start.1
  396.3 1.2 copy.14
  397.5 0.9 copy-done.1
  398.4 0.0 copy-start
  398.4 1.2 copy.15
  399.7 0.9 copy-done
  400.6 1.2 copy.16
Async XLA Ops:
  391.5 4.8 %copy-start.2 = (bf16[2,128,3584]{2,1,0:T(8,128)(2,1)S(1)}, bf16[2,128,3584]{2,1,0:T(8,128)(2,1)}, u32[]{:S(2)}) copy-start(bf16[2,128,3584]{2,1,0:T(8,128)(2,1)} %get-tuple-element.17) | copy-start | bytes 5505028
  396.3 2.2 copy-start.1
  398.4 2.2 copy-start

commit v3 on v2

v3 whole, which is shorter than its diff:
```python
import functools

import jax
import jax.numpy as jnp
from jax import lax
from jax.experimental import pallas as pl
from jax.experimental.pallas import tpu as pltpu
from jax.sharding import PartitionSpec as P

BF, F32 = jnp.bfloat16, jnp.float32
MESH = pl.DeviceIdType.MESH
CORES = 2
BW = 128
TILES = 2
SUB = 4
G_, U_, D_ = 0, 1, 2


def dot(a, b, ca=1, cb=0):
    return lax.dot_general(a, b, (((ca,), (cb,)), ((), ())), preferred_element_type=F32)


def when(condition, f):
    if isinstance(condition, bool):
        if condition:
            f()
    else:
        pl.when(condition)(f)


def kernel(dims, x_ref, dy_ref, wg_ref, wu_ref, wd_ref,
           by_x, og, ou, od, G, WDO, ST, PT, A0T, H1, DGU,
           a_nat, a_t, dyv, acc, wbuf, dgu, pt, stb, own_v,
           s_send, d_recv, own32, r32, l32, s_u1, s_pr, s_pl, u2r, u2l, ra, rb, rc, rd, v, ya, yb, yc, f_out,
           g_send, g_recv, w_sem, st_sem, pt_sem, ld_sem, rs_send, d_sem, x_sem, rc_sem, ys_sem, yr_sem, o_sem, od_send, od_recv,
           own_sem, own_out, ex_send, ex_recv, dg_sem):
    nx, ny, C, T, D = dims
    TM = T // TILES
    N = 2 * C
    DR = D // (CORES * nx)
    HR, QR = DR // 2, DR // 4
    CW = nx * BW
    DH = D // 2

    s, y = lax.axis_index("s"), lax.axis_index("r")
    X, k = lax.div(s, CORES), lax.rem(s, CORES)
    at = lambda xx, kk: CORES * lax.rem(xx, nx) + kk
    right, left = {"s": at(X + 1, k)}, {"s": at(X + nx - 1, k)}
    sib = {"s": at(X, 1 - k)}
    up, down = {"r": lax.rem(y + 1, ny)}, {"r": lax.rem(y + ny - 1, ny)}

    def remote(src, dst, ss, rs, who):
        return pltpu.make_async_remote_copy(src_ref=src, dst_ref=dst, send_sem=ss, recv_sem=rs, device_id=who, device_id_type=MESH)

    def arrived(dst, rs):
        pltpu.make_async_copy(dst, dst, rs).wait()

    pL, pR, pO = at(X + nx - 1, k), at(X + 1, k), at(X + 2, k)
    others = (at(X + nx - 1, 1 - k), at(X + 1, 1 - k), at(X + 2, 1 - k), at(X, 1 - k))
    par = lax.rem(y, 2)
    mine, other = par * HR, (1 - par) * HR

    def rows(base, q):
        return pl.ds(pl.multiple_of(base + q * QR, QR), QR)

    PARTS = {None: pl.ds(0, 3), 0: pl.ds(0, 2), 1: pl.ds(2, 1)}

    def out_copy(t, n, part=None):
        full = pl.ds(0, DR)
        spec = {
            0: (None, rows(mine, 0), right), 1: (None, rows(mine, 1), right),
            2: (None, rows(mine, 1), left), 3: (None, rows(mine, 0), left),
            4: (pL, rows(mine, 0), right), 5: (pR, rows(mine, 1), left),
            6: (pL, rows(mine, 0), up), 7: (pR, rows(mine, 0), up), 8: (pO, rows(mine, 0), up),
            9: (pL, rows(mine, 1), down), 10: (pR, rows(mine, 1), down), 11: (pO, rows(mine, 1), down),
            12: (None, full, sib), 13: (pL, full, sib), 14: (pR, full, sib), 15: (pO, full, sib),
        }
        j, r, who = spec[t]
        q = PARTS[part]
        src = own_v.at[lax.rem(n, 4), q, r, :] if j is None else G.at[n, q, j, r, :]
        dst = G.at[n, q, s if j is None else j, r, :]
        leaves = g_send.at[lax.rem(n, 4), 0 if j is None else 1]
        return remote(src, dst, leaves, g_recv.at[8 if part == 1 else lax.rem(n, 8), STAGE[t]], who)

    STAGE = (0, 1, 0, 1, 2, 2, 3, 3, 3, 3, 3, 3, 4, 4, 4, 4)

    def in_wait(i, n, part=None):
        q = PARTS[part]
        to = (G.at[n, q, 0, pl.ds(0, HR)],) * 3 + (G.at[n, q, pl.ds(0, 3), pl.ds(0, HR)], G.at[n, q, pl.ds(0, 4)])
        arrived(to[i], g_recv.at[8 if part == 1 else lax.rem(n, 8), i])

    def left_own(n):
        arrived(G.at[n, :, pl.ds(0, 2)], g_send.at[lax.rem(n, 4), 0])

    def left_passed(n):
        arrived(G.at[n, :, pl.ds(0, 5)], g_send.at[lax.rem(n, 4), 1])

    def named(f):
        def run(*args):
            with jax.named_scope(f.__name__):
                return f(*args)
        return run

    def stage(f):
        return lambda n, *part: when((n >= 0) & (n < N) if not isinstance(n, int) else 0 <= n < N, lambda: named(f)(n, *part))

    def starts(n, part, *ts):
        for t in ts:
            out_copy(t, n, part).start()

    def layer_of(n):
        if isinstance(n, int):
            return n // C, n % C
        second = n >= C
        return jnp.where(second, 1, 0), jnp.where(second, n - C, n)

    def block_cols(j, c):
        return pl.ds(pl.multiple_of((j * C + c) * BW, BW), BW)

    def half_block(h):
        o = jnp.where(h >= C, 1, 0)
        return o, pl.ds(pl.multiple_of(HR * (h - C * o), HR), HR)

    def core_cols(core):
        return pl.ds(pl.multiple_of(core * DH, DH), DH)

    def exchange(layer):
        mine_ = pl.ds(pl.multiple_of(k * C * HR, HR), C * HR)
        return remote(wd_ref.at[layer, :, core_cols(1 - k)], WDO.at[layer, mine_], ex_send.at[layer], ex_recv.at[layer], sib)

    def exchanged(layer):
        theirs = pl.ds(pl.multiple_of((1 - k) * C * HR, HR), C * HR)
        arrived(WDO.at[layer, theirs], ex_recv.at[layer])

    def own_down(n, sem):
        slot, (layer, c) = lax.rem(n, 4), layer_of(n)
        for e in range(2):
            h = 2 * c + e
            o, r = half_block(h)
            dst = own_v.at[slot, D_, pl.ds(e * HR, HR)]
            far = pl.ds(pl.multiple_of(HR * h, HR), HR)
            pl.when(o == k)(lambda: pltpu.make_async_copy(wd_ref.at[layer, r, core_cols(k)], dst, sem).start())
            pl.when(o != k)(lambda: pltpu.make_async_copy(WDO.at[layer, far], dst, sem).start())

    def own_cols(n):
        slot, (layer, c) = lax.rem(n, 4), layer_of(n)
        for q, w in ((G_, wg_ref), (U_, wu_ref)):
            for j in range(nx):
                pltpu.make_async_copy(w.at[layer, :, block_cols(j, c)], own_v.at[slot, q, :, pl.ds(j * BW, BW)], own_sem.at[slot]).start()

    @stage
    def gS(n):
        when(n >= 4, lambda: left_own(n - 4))
        own_cols(n)
        own_down(n, own_sem.at[lax.rem(n, 4)])

    def own_stored(n):
        return pltpu.make_async_copy(own_v.at[lax.rem(n, 4)], G.at[n, :, s], own_out.at[lax.rem(n, 4)])

    @stage
    def gA(n):
        slot = lax.rem(n, 4)
        pltpu.make_async_copy(own_v.at[slot], own_v.at[slot], own_sem.at[slot]).wait()
        starts(n, None, 0, 2, 1, 3, 12)
        own_stored(n).start()

    @stage
    def gB(n, part=None):
        when(n >= 4, lambda: left_passed(n - 4))
        in_wait(0, n, part)
        starts(n, part, 4, 5, 6, 10)

    @stage
    def gC(n, part=None):
        in_wait(1, n, part)
        starts(n, part, 9, 7)

    @stage
    def gD(n, part=None):
        in_wait(2, n, part)
        starts(n, part, 8, 11)

    @stage
    def gE(n, part=None):
        in_wait(3, n, part)
        starts(n, part, 13, 14, 15)
        if part != 1:
            own_stored(n).wait()

    def load(n, packets, *parts):
        slot = lax.rem(n, 2)
        for part in parts:
            q = PARTS[part]
            for p in packets:
                pltpu.make_async_copy(G.at[n, q, p], wbuf.at[slot, q, p], w_sem.at[slot, part]).start()

    def wait_weights(slot, part):
        to = wbuf.at[slot, PARTS[part]]
        pltpu.make_async_copy(to, to, w_sem.at[slot, part]).wait()

    @stage
    def gL(n, *parts):
        load(n, (s, pL, pR, pO), *(parts or (0, 1)))

    @stage
    def gF(n, part=None):
        in_wait(4, n, part)
        load(n, others, *((0, 1) if part is None else (part,)))

    def w_cols(slot, q):
        return wbuf[slot, q].reshape(D, CW)

    def w_half(slot, q, h):
        return wbuf[slot, q, pl.ds(h * nx, nx)].reshape(DH, CW)

    def wd_half(slot, h):
        return jnp.concatenate([wbuf[slot, D_, CORES * j + h] for j in range(nx)], axis=0)

    def tile(i, n=None):
        n = TM if n is None else n
        return pl.ds(pl.multiple_of(i * n, n), n)

    def rel(j):
        return lax.rem(X + j, nx)

    def lane_lhs(lane):
        return jnp.concatenate([a_t[rel(j), lane] for j in range(nx)], axis=0)

    def grad(q, lane):
        if q == D_:
            lhs = jnp.concatenate([pt[rel(j)] for j in range(nx)], axis=0)
            return dot(lhs, dyv[lane])
        return dot(lane_lhs(lane), dgu[q])

    def d_copy(q, m):
        return remote(s_send.at[q], d_recv.at[lax.rem(m, 2), q], rs_send.at[0], d_sem.at[lax.rem(m, 2)], sib)

    def send_lane(q, m):
        s_send[q] = grad(q, 1 - k).astype(BF).reshape(nx, DR, CW)

    @named
    def send_lanes(m):
        when(m > 0, lambda: arrived(s_send, rs_send.at[0]))
        send_lane(D_, m)
        send_lane(G_, m)
        d_copy(D_, m).start()
        d_copy(G_, m).start()
        send_lane(U_, m)
        d_copy(U_, m).start()

    lo, hi = pl.ds(0, HR), pl.ds(HR, HR)

    one, two_ = v.at[0], v.at[pl.ds(0, 2)]

    def x_copy(t, m):
        two, three = lax.rem(m, 2), lax.rem(m, 3)
        src, dst, sem, who = {
            0: (s_u1.at[:, lo], ra.at[two], x_sem.at[two], right),
            1: (s_u1.at[:, hi], rb.at[two], x_sem.at[two], left),
            2: (s_pr, rc.at[three, :, hi], rc_sem.at[three], right),
            3: (s_pl, rd.at[three, :, lo], rc_sem.at[three], left),
            4: (u2r, rc.at[three, :, lo], rc_sem.at[three], right),
            5: (u2l, rd.at[three, :, hi], rc_sem.at[three], left),
        }[t]
        return remote(src, dst, rs_send.at[1 if t < 4 else 2], sem, who)

    def y_copy(t, m):
        three = lax.rem(m, 3)
        src, dst, who = {
            0: (v.at[three, :, lo], ya.at[three, :, lo], up),
            1: (v.at[three, :, hi], ya.at[three, :, hi], up),
            2: (v.at[three, :, hi], yb.at[three, :, hi], down),
            3: (v.at[three, :, lo], yb.at[three, :, lo], down),
            4: (ya.at[three, :, lo], yc.at[three, :, lo], up),
            5: (yb.at[three, :, hi], yc.at[three, :, hi], down),
        }[t]
        return remote(src, dst, ys_sem.at[three], yr_sem.at[three, 0 if t in (0, 2) else 1], who)

    @named
    def keep_lanes(m):
        two = lax.rem(m, 2)

        when(m > 0, lambda: arrived(two_, rs_send.at[1]))
        when(m >= 3, lambda: y3_wait(m - 3))
        arrived(d_recv.at[two], d_sem.at[two])
        for q in (D_, G_, U_):
            if q == G_:
                y3_add(m - 3)
            total = (grad(q, k) + d_recv[two, q].reshape(CW, CW).astype(F32)).reshape(nx, DR, CW)
            own32[two, q] = total[0]
            r32[q] = total[1, :HR]
            s_pr[q] = total[1, HR:].astype(BF)
            s_u1[q] = total[2].astype(BF)
            s_pl[q] = total[3, :HR].astype(BF)
            l32[q] = total[3, HR:]

    @named
    def x1(m):
        for t in range(4):
            x_copy(t, m).start()

    def slot_of(m, n):
        return lax.rem(m + n, n)

    @named
    def x2_wait(m):
        arrived(one, x_sem.at[lax.rem(m, 2)])
        when(m > 0, lambda: arrived(one, rs_send.at[2]))

    def x2_add(m):
        two = slot_of(m, 2)
        for q in range(3):
            u2r[q] = (r32[q] + ra[two, q].astype(F32)).astype(BF)
            u2l[q] = (l32[q] + rb[two, q].astype(F32)).astype(BF)

    def x2_out(m):
        x_copy(4, m).start()
        x_copy(5, m).start()

    def x2(m):
        x2_wait(m)
        x2_add(m)
        x2_out(m)

    @named
    def x3(m):
        arrived(two_, rc_sem.at[lax.rem(m, 3)])
        two, three = lax.rem(m, 2), lax.rem(m, 3)
        for q in range(3):
            v[three, q] = (own32[two, q] + rc[three, q].astype(F32) + rd[three, q].astype(F32)).astype(BF)
        for t in (0, 2, 1, 3):
            y_copy(t, m).start()

    @named
    def y2(m):
        arrived(one, yr_sem.at[lax.rem(m, 3), 0])
        y_copy(4, m).start()
        y_copy(5, m).start()

    def where_m(m):
        first = m < C
        return jnp.where(first, 1, 0), jnp.where(first, m, m - C)

    def cols_out(q, m):
        layer, c = where_m(m)
        return [pltpu.make_async_copy(f_out.at[q, :, pl.ds(j * BW, BW)], (og, ou)[q].at[layer, :, block_cols(j, c)], o_sem.at[q])
                for j in range(nx)]

    def od_each(m, local, far):
        layer, c = where_m(m)
        for e in range(2):
            o, r = half_block(2 * c + e)
            src, dst = f_out.at[D_, pl.ds(e * HR, HR)], od.at[layer, r, core_cols(k)]
            pl.when(o == k)(functools.partial(local, pltpu.make_async_copy(src, dst, o_sem.at[2 + e])))
            pl.when(o != k)(functools.partial(far, remote(src, dst, od_send.at[e], od_recv, sib)))

    @named
    def out_done(m):
        for q in (G_, U_):
            pltpu.make_async_copy(f_out.at[q], f_out.at[q], o_sem.at[q]).wait()
        od_each(m, lambda c: c.wait(), lambda c: c.wait_send())

    @named
    def y3_wait(m):
        arrived(two_, yr_sem.at[lax.rem(m, 3), 1])
        when(m > 0, lambda: out_done(m - 1))

    def y3_add(m):
        three = slot_of(m, 3)
        for q in range(3):
            a = v[three, q].astype(F32) + yc[three, q].astype(F32)
            b = ya[three, q].astype(F32) + yb[three, q].astype(F32)
            f_out[q] = (a + b).astype(BF)

    @named
    def y3_out(m):
        arrived(v, ys_sem.at[lax.rem(m, 3)])
        for q in (G_, U_):
            for c_ in cols_out(q, m):
                c_.start()
        od_each(m, lambda c: c.start(), lambda c: c.start())

    def y3(m):
        y3_wait(m)
        y3_add(m)
        y3_out(m)

    def lagged(f, m):
        when(m >= 0, lambda: f(m))

    def halves(src, dst, r, sem):
        return [pltpu.make_async_copy(src.at[r, pl.ds(h * DH, DH)], dst.at[h, r], sem) for h in range(2)]

    every = pl.ds(0, T)
    own_cols(0)
    for c_ in halves(x_ref.at[0], dyv, every, ld_sem.at[0]):
        c_.start()

    barrier = pltpu.get_barrier_semaphore()
    for who in (right, left, sib, up, down):
        pl.semaphore_signal(barrier, inc=1, device_id=who, device_id_type=MESH)
    with jax.named_scope("entry"):
        pl.semaphore_wait(barrier, 5)

    for layer in range(2):
        exchange(layer).start()
    first = own_v.at[0, PARTS[0]]
    with jax.named_scope("own_wait"):
        pltpu.make_async_copy(first, first, own_sem.at[0]).wait()
    starts(0, 0, 0, 2, 1, 3, 12)
    own_cols(1)
    named(exchanged)(0)
    own_down(0, ld_sem.at[2])
    own_down(1, own_sem.at[1])
    pltpu.make_async_copy(dyv, dyv, ld_sem.at[0]).wait()

    NT = 4 * TILES
    TN = T // NT

    def both(ref, r):
        return jnp.concatenate([ref[0, r, :], ref[1, r, :]], axis=1)

    def put_a(h, i):
        r = tile(i, TN)
        scale = lax.rsqrt(jnp.mean(h * h, -1, keepdims=True) + 1e-6)
        a = (h * scale).astype(BF)
        a_nat[r, :] = a
        a_t[:, :, :, r] = a.T.reshape(nx, CORES, DR, TN)

    def norm0(i, _):
        r = tile(i, TN)
        put_a(both(dyv, r).astype(F32), i)
        acc[r, :] = jnp.zeros((TN, D), F32)
        return _

    lax.fori_loop(0, NT // 4, norm0, 0)
    first = own_v.at[0, PARTS[1]]
    pltpu.make_async_copy(first, first, ld_sem.at[2]).wait()
    starts(0, 1, 0, 2, 1, 3, 12)
    own_stored(0).start()
    lax.fori_loop(NT // 4, NT, norm0, 0)
    a0t_out = pltpu.make_async_copy(a_t, A0T, ld_sem.at[1])
    a0t_out.start()
    gB(0, 0)
    gC(0, 0)
    gB(0, 1)
    gC(0, 1)
    gA(1)
    exchanged(1)
    gS(2)
    gD(0, 0)
    gD(0, 1)
    gB(1)
    gA(2)
    gS(3)
    gE(0, 0)
    gL(0, 0)
    gC(1)
    gE(0, 1)
    gL(0, 1)
    gF(0, 0)

    A, B, C_, D__, E, F, L = gA, gB, gC, gD, gE, gF, gL
    fwd_hooks = {
        (0, 0): [(F, 0, 1), (D__, 1), (B, 2)], (0, 1): [(C_, 2), (A, 3)], (0, 2): [(E, 1), (L, 1), (D__, 2)], (0, 3): [(B, 3), (F, 1)],
        (1, 0): [(C_, 3), (E, 2), (L, 2), (A, 4)], (1, 1): [(D__, 3)], (1, 2): [(F, 2), (B, 4)], (1, 3): [(C_, 4), (E, 3), (A, 5)],
        (2, 0): [(L, 3)], (2, 1): [(D__, 4)], (2, 2): [(F, 3), (B, 5)], (2, 3): [(C_, 5), (E, 4), (A, 6)],
        (3, 0): [(L, 4)], (3, 1): [(D__, 5)], (3, 2): [(F, 4), (B, 6)], (3, 3): [(C_, 6), (E, 5), (A, 7)],
        (4, 0): [(L, 5)], (4, 1): [(D__, 6)], (4, 2): [(F, 5), (B, 7)], (4, 3): [(C_, 7), (E, 6), (A, 8)],
        (5, 0): [(L, 6)], (5, 1): [(D__, 7)], (5, 2): [(F, 6), (B, 8)], (5, 3): [(C_, 8), (E, 7), (A, 9)],
        (6, 0): [(L, 7)], (6, 1): [(D__, 8)], (6, 2): [(F, 7), (B, 9)], (6, 3): [(C_, 9), (E, 8), (A, 10)],
    }

    def fwd_hook(h, c):
        for (at_c, at_h), todo in fwd_hooks.items():
            if at_h == h:
                @pl.when(c == at_c)
                def _(todo=todo):
                    for f, *n in todo:
                        f(*n)
                        if f is gA and n[0] + 1 < N:
                            gS(n[0] + 1)

    def st_out(tau):
        i = lax.rem(tau, TILES)
        return pltpu.make_async_copy(stb.at[i], ST.at[tau], st_sem.at[i])

    def pt_out(c, i):
        cols = tile(i)
        return pltpu.make_async_copy(pt.at[:, :, cols], PT.at[c, :, :, cols], pt_sem.at[i])

    def gate_up(slot, r):
        a = a_nat[r, :]
        g, u = dot(a, w_cols(slot, G_)), dot(a, w_cols(slot, U_))
        sig = jax.nn.sigmoid(g)
        silu = g * sig
        return silu, u * (sig + silu * (1.0 - sig)), (silu * u).astype(BF)

    def put_pt(p, i):
        pt[:, :, tile(i, TM // SUB)] = p.T.reshape(nx, BW, TM // SUB)

    def fwd(c, carry):
        slot = lax.rem(c, 2)
        wait_weights(slot, 0)

        fwd_hook(0, c)

        def up_tile(i, _):
            pl.when(i == 1)(lambda: fwd_hook(1, c))

            @pl.when(c >= 1)
            def stored():
                st_out(TILES * (c - 1) + i).wait()
                pt_out(c - 1, i).wait()

            with jax.named_scope("fwd_up"):
                for j in range(SUB):
                    e = SUB * i + j
                    r = tile(e, TM // SUB)
                    silu, slope, p = gate_up(slot, r)
                    inner = pl.ds(j * (TM // SUB), TM // SUB)
                    stb[i, 0, inner] = silu
                    stb[i, 1, inner] = slope
                    put_pt(p, e)
                    dgu[0, r, :] = p
            st_out(TILES * c + i).start()
            pt_out(c, i).start()
            return _

        lax.fori_loop(0, TILES, up_tile, 0)
        fwd_hook(2, c)
        wait_weights(slot, 1)

        @pl.when(c < C - 1)
        def _():
            with jax.named_scope("fwd_down"):
                for h in range(2):
                    acc[:, h * DH:(h + 1) * DH] += dot(dgu[0], wd_half(slot, h))

        @pl.when(c == C - 1)
        def _():
            a0t_out.wait()

            def one(j, _):
                with jax.named_scope("fwd_last"):
                    for e in range(NT // 2):
                        i = NT // 2 * j + e
                        r = tile(i, TN)
                        total = acc[r, :] + jnp.concatenate([dot(dgu[0, r, :], wd_half(slot, h)) for h in range(2)], axis=1)
                        h = (both(dyv, r).astype(F32) + total.astype(BF).astype(F32)).astype(BF)
                        for g in range(2):
                            dgu[g, r, :] = h[:, g * DH:(g + 1) * DH]
                        put_a(h.astype(F32), i)
                        acc[r, :] = jnp.zeros((TN, D), F32)
                r = tile(j, T // 2)
                for g in range(2):
                    pltpu.make_async_copy(dgu.at[g, r], H1.at[g, r], ld_sem.at[2]).start()
                for c_ in halves(dy_ref.at[0], dyv, r, ld_sem.at[0]):
                    c_.start()
                return _

            lax.fori_loop(0, 2, one, 0)

        fwd_hook(3, c)
        return carry

    lax.fori_loop(0, C, fwd, 0)
    for i in range(TILES):
        st_out(TILES * (C - 1) + i).wait()
        pt_out(C - 1, i).wait()
    pltpu.make_async_copy(dgu, H1, ld_sem.at[2]).wait()
    pltpu.make_async_copy(dyv, dyv, ld_sem.at[0]).wait()

    def d_p(slot, r):
        return dot(dyv[0, r, :], wd_half(slot, 0), 1, 1) + dot(dyv[1, r, :], wd_half(slot, 1), 1, 1)

    def put_d(r, dp, silu, slope):
        dgu[G_, r, :] = (dp * slope).astype(BF)
        dgu[U_, r, :] = (dp * silu).astype(BF)

    h1_in = [pltpu.make_async_copy(H1.at[h], a_nat.at[:, pl.ds(h * DH, DH)], ld_sem.at[0]) for h in range(2)]
    a0t_in = pltpu.make_async_copy(A0T, a_t, ld_sem.at[1])
    x_in = pltpu.make_async_copy(x_ref.at[0], a_nat, ld_sem.at[2])

    def st_load(c):
        for i in range(TILES):
            for e in range(2):
                pltpu.make_async_copy(ST.at[TILES * c + i, e], stb.at[i, e], st_sem.at[i]).start()

    def st_wait(i):
        pltpu.make_async_copy(stb.at[i], stb.at[i], st_sem.at[i]).wait()

    def pt_in(c):
        return pltpu.make_async_copy(PT.at[c], pt, pt_sem.at[0])

    def norm_back(h, d, through):
        scale = lax.rsqrt(jnp.mean(h * h, -1, keepdims=True) + 1e-6)
        along = jnp.sum(d * h, -1, keepdims=True) * (scale * scale * scale) * (1.0 / D)
        return (through + (d * scale - h * along)).astype(BF)

    def middle():
        pltpu.make_async_copy(a_nat, a_nat, ld_sem.at[0]).wait()

        def mid(i, _):
            with jax.named_scope("mid"):
                r = tile(i, TN)
                out = norm_back(a_nat[r, :].astype(F32), acc[r, :], both(dyv, r).astype(F32))
                for e in range(2):
                    dyv[e, r, :] = out[:, e * DH:(e + 1) * DH]
                acc[r, :] = jnp.zeros((TN, D), F32)
            return _

        lax.fori_loop(0, NT, mid, 0)
        x_in.start()
        a0t_in.wait()

    at_hook = {
        0: {0: [(gD, 2), (gA, 4), (gS, 5)], 1: [(gD, 4), (gB, 5), (gC, 5), (gE, 3), (gA, 6)], 2: [(gB, 6), (gC, 6)], 3: [(gE, 6)]},
        2: {0: [(gB, 3), (gC, 3), (gE, 2), (gB, 4), (gC, 4), (gA, 5), (gS, 6)], 1: [(gE, 4)], 2: [(gE, 5)]},
        3: {},
        4: {0: [(gD, 3)], 1: [(gD, 5)], 2: [(gD, 6)]},
    }

    def hook(h, m):
        for step, todo in at_hook[h].items():
            @pl.when(m == step)
            def _(todo=todo):
                for f, n in todo:
                    f(C + n)

    def dg_out(c):
        return pltpu.make_async_copy(dgu.at[:, pl.ds(T // 2, T // 2)], DGU.at[c], dg_sem.at[0])

    def d_a(slot, to, base):
        with jax.named_scope("da_tile"):
            r = pl.ds(base, T // 2)
            for h in range(2):
                acc[to:to + T // 2, h * DH:(h + 1) * DH] += (
                    dot(dgu[G_, r, :], w_half(slot, G_, h), 1, 1) + dot(dgu[U_, r, :], w_half(slot, U_, h), 1, 1))

    def bwd(m, carry):
        slot = lax.rem(m + 1, 2)
        last = m == C - 1
        first_layer = m >= C
        pl.when(m == C)(middle)
        wait_weights(slot, 1)

        @pl.when(first_layer & (m < 2 * C - 1))
        def _():
            load(m + 1 - C, range(CORES * nx), 0, 1)

        hook(0, m)

        @pl.when(jnp.logical_not(first_layer))
        def _():
            wait_weights(slot, 0)

            with jax.named_scope("bwd1_tile"):
                for e in range(TILES * SUB):
                    r = tile(e, TM // SUB)
                    silu, slope, p = gate_up(slot, r)
                    put_pt(p, e)
                    put_d(r, d_p(slot, r), silu, slope)

        @pl.when(first_layer)
        def _():
            pl.when(m > C)(lambda: dg_out(m - 1 - C).wait())
            for i in range(TILES):
                st_wait(i)
            with jax.named_scope("bwd0_tile"):
                for e in range(TILES * SUB):
                    r = pl.ds(e * (TM // SUB), TM // SUB)
                    inner = pl.ds((e % SUB) * (TM // SUB), TM // SUB)
                    put_d(r, d_p(slot, r), stb[e // SUB, 0, inner], stb[e // SUB, 1, inner])
            pl.when(m < 2 * C - 1)(lambda: dg_out(m - C).start())
            pt_in(m - C).wait()

        hook(2, m)
        lagged(x3, m - 2)

        @pl.when(last)
        def _():
            for c_ in h1_in:
                c_.start()
            load(0, range(CORES * nx), 0, 1)

        @pl.when((m >= C - 1) & (m < 2 * C - 1))
        def _():
            st_load(m + 1 - C)

        send_lanes(m)
        hook(3, m)

        @pl.when(m < C - 1)
        def _():
            gL(C + 1 + m)
            gF(C + 1 + m)

        pl.when(first_layer)(lambda: wait_weights(slot, 0))
        d_a(slot, 0, 0)
        lagged(x2, m - 1)
        hook(4, m)
        keep_lanes(m)
        x1(m)
        lagged(y2, m - 2)
        when(m >= 3, lambda: y3_out(m - 3))
        pl.when((m >= C - 1) & (m < 2 * C - 1))(lambda: pt_in(m + 1 - C).start())
        pl.when(last)(a0t_in.start)
        pl.when(m < C)(lambda: d_a(slot, T // 2, T // 2))
        return carry

    lax.fori_loop(0, 2 * C, bwd, 0)

    M = 2 * C

    def dg_in(c, half):
        return pltpu.make_async_copy(DGU.at[c], dgu.at[:, pl.ds(half * (T // 2), T // 2)], dg_sem.at[half])

    def late(j, carry):
        slot, half = lax.rem(j, 2), 1 - lax.rem(j, 2)

        @pl.when(j >= 1)
        def _():
            wait_weights(slot, 0)
            dg_in(j - 1, half).wait()

        @pl.when(j < C - 1)
        def _():
            for p in range(CORES * nx):
                pltpu.make_async_copy(G.at[j, PARTS[0], p], wbuf.at[1 - slot, PARTS[0], p], w_sem.at[1 - slot, 0]).start()
            dg_in(j, 1 - half).start()

        d_a(slot, T // 2, pl.multiple_of(half * (T // 2), T // 2))
        pl.when(j == 0)(lambda: x3(M - 2))
        pl.when(j == C - 6)(lambda: x2(M - 1))
        pl.when(j == C - 4)(lambda: y2(M - 2))
        pl.when(j == C - 3)(lambda: x3(M - 1))
        pl.when(j == C - 2)(lambda: y3(M - 3))
        return carry

    lax.fori_loop(0, C, late, 0)

    x_in.wait()

    def by_out(i):
        r = tile(i, TN)
        return pltpu.make_async_copy(a_nat.at[r], by_x.at[0, r], ld_sem.at[0])

    def last_norm(i, _):
        r = tile(i, TN)
        a_nat[r, :] = norm_back(a_nat[r, :].astype(F32), acc[r, :], both(dyv, r).astype(F32))
        by_out(i).start()
        return _

    lax.fori_loop(0, NT // 2, last_norm, 0)
    y2(M - 1)
    lax.fori_loop(NT // 2, NT, last_norm, 0)
    y3(M - 2)

    arrived(s_send, rs_send.at[0])
    arrived(two_, rs_send.at[1])
    arrived(one, rs_send.at[2])
    for layer in range(2):
        exchange(layer).wait_send()
    for n in range(N - 4, N):
        left_own(n)
        left_passed(n)
    pltpu.make_async_copy(a_nat, by_x.at[0], ld_sem.at[0]).wait()
    y3(M - 1)
    out_done(M - 1)
    arrived(od.at[:, :, pl.ds(0, DH)], od_recv)


def solution(mesh):
    nx, ny = mesh.shape["s"] // CORES, mesh.shape["r"]

    def step(x, dy, w_gate, w_up, w_down):
        layers, dr, ff = w_gate.shape
        _, T, D = x.shape
        C = ff // (nx * BW)
        N, CW, DH, HR = layers * C, nx * BW, D // 2, dr // 2
        TM = T // TILES

        hbm = pl.BlockSpec(memory_space=pltpu.HBM)
        shape = jax.ShapeDtypeStruct
        outs = pl.pallas_call(
            functools.partial(kernel, (nx, ny, C, T, D)),
            out_shape=[
                shape((1, T, D), BF), shape(w_gate.shape, BF), shape(w_up.shape, BF), shape(w_down.shape, BF),
                shape((N, 3, CORES * nx, dr, CW), BF), shape((layers, C * BW, DH), BF),
                shape((TILES * C, 2, TM, CW), F32), shape((C, nx, BW, T), BF),
                shape((nx, CORES, dr, T), BF), shape((2, T, DH), BF), shape((C, 2, T // 2, CW), BF),
            ],
            in_specs=[hbm] * 5,
            out_specs=[hbm] * 11,
            scratch_shapes=[
                pltpu.VMEM((T, D), BF), pltpu.VMEM((nx, CORES, dr, T), BF), pltpu.VMEM((2, T, DH), BF), pltpu.VMEM((T, D), F32),
                pltpu.VMEM((2, 3, CORES * nx, dr, CW), BF), pltpu.VMEM((2, T, CW), BF), pltpu.VMEM((nx, BW, T), BF),
                pltpu.VMEM((TILES, 2, TM, CW), F32), pltpu.VMEM((4, 3, dr, CW), BF),
                pltpu.VMEM((3, nx, dr, CW), BF), pltpu.VMEM((2, 3, nx, dr, CW), BF), pltpu.VMEM((2, 3, dr, CW), F32),
                pltpu.VMEM((3, HR, CW), F32), pltpu.VMEM((3, HR, CW), F32), pltpu.VMEM((3, dr, CW), BF),
                pltpu.VMEM((3, HR, CW), BF), pltpu.VMEM((3, HR, CW), BF), pltpu.VMEM((3, HR, CW), BF), pltpu.VMEM((3, HR, CW), BF),
                pltpu.VMEM((2, 3, HR, CW), BF), pltpu.VMEM((2, 3, HR, CW), BF),
                pltpu.VMEM((3, 3, dr, CW), BF), pltpu.VMEM((3, 3, dr, CW), BF), pltpu.VMEM((3, 3, dr, CW), BF),
                pltpu.VMEM((3, 3, dr, CW), BF), pltpu.VMEM((3, 3, dr, CW), BF), pltpu.VMEM((3, 3, dr, CW), BF),
                pltpu.VMEM((3, dr, CW), BF),
                *(pltpu.SemaphoreType.DMA(n) for n in (
                    (4, 2), (9, 5), (2, 2), (2,), (TILES,), (3,), (3,), (2,), (2,), (3,), (3,), (3, 2), (4,), (2,), (), (4,), (4,), (2,), (2,), (2,))),
            ],
            compiler_params=pltpu.CompilerParams(collective_id=0, has_side_effects=True, vmem_limit_bytes=67043328),
            name="stack",
        )(x, dy, w_gate, w_up, w_down)
        return tuple(outs[:4])

    states, cut = P(("rep", "r", "s"), None, None), P(None, "s", None)
    return jax.shard_map(
        step,
        mesh=mesh,
        in_specs=(states, states) + (cut,) * 3,
        out_specs=(states,) + (P("rep", "s", None),) * 3,
        check_vma=False,
    )
```

time: 402 us -> 370 us (0.920)
  Pallas kernels: 391 us -> 360 us
    pallas_call x1, Pallas kernels: 391 us -> 360 us  [step(): pl.pallas_call(functools.partial(kernel, (nx, ny, C, T, D)), out_shape=[s...]
where the time goes in v3:
time: 370 us; the launch traced here: 369 us
  Pallas kernels  360 us (97%)
  local copies, waits for them, and re-layouts  8.51 us (2%)
    pallas_call x1, Pallas kernels, step(): pl.pallas_call(functools.partial(kernel, (nx, ny, C, T, D)), out_shape=[s...  360 us
    unnamed x10, local copies, waits for them, and re-layouts  8.51 us

profile of v3, /device:TPU:97, one launch (start us, length us, event | category | flops | bytes accessed | tf_op | source)
XLA Modules:
  0.0 369.3 jit_solution(7467951661793246286)
XLA Ops:
  0.6 360.2 %stack.1 = (bf16[1,2048,1024]{2,1,0:T(8,128)(2,1)}, bf16[2,128,3584]{2,1,0:T(8,128)(2,1)}, bf16[2,128,3584]{2,1,0:T(8,128)(2,1)}, bf16[2,448,1024]{2,1,0:T(8,128...) custom-call(bf16[1,2048,1024]{2,1,0:T(8,128)(2,1)} %x_ref.1, ...), custom_call_target="tpu_custom_call" | custom-call | tf_op jit(solution)/shard_map/stack/pallas_call | solution.py:786
  360.8 0.0 copy-start.2
  360.8 0.0 copy-start.1
  360.8 4.8 %copy.13 = bf16[1,2048,1024]{2,1,0:T(8,128)(2,1)} copy(bf16[1,2048,1024]{2,1,0:T(8,128)(2,1)} %get-tuple-element.16) | data formatting | bytes 8388608
  365.6 0.0 copy-done.2
  365.6 0.0 copy-start
  365.6 1.2 copy.14
  366.9 0.0 copy-done.1
  366.9 1.2 copy.15
  368.1 0.0 copy-done
  368.1 1.2 copy.16
Async XLA Ops:
  360.8 4.8 %copy-start.2 = (bf16[2,128,3584]{2,1,0:T(8,128)(2,1)S(1)}, bf16[2,128,3584]{2,1,0:T(8,128)(2,1)}, u32[]{:S(2)}) copy-start(bf16[2,128,3584]{2,1,0:T(8,128)(2,1)} %get-tuple-element.17) | copy-start | bytes 5505028
  360.8 6.1 %copy-start.1 = (bf16[2,128,3584]{2,1,0:T(8,128)(2,1)S(1)}, bf16[2,128,3584]{2,1,0:T(8,128)(2,1)}, u32[]{:S(2)}) copy-start(bf16[2,128,3584]{2,1,0:T(8,128)(2,1)} %get-tuple-element.18) | copy-start | bytes 5505028
  365.6 2.5 copy-start

commit v4 on v3

--- a/solution.py
+++ b/solution.py
@@ -12,6 +12,7 @@
 CORES = 2
 BW = 128
 TILES = 2
+NH = 256
 SUB = 4
 G_, U_, D_ = 0, 1, 2
 
@@ -55,8 +56,8 @@
     def arrived(dst, rs):
         pltpu.make_async_copy(dst, dst, rs).wait()
 
-    pL, pR, pO = at(X + nx - 1, k), at(X + 1, k), at(X + 2, k)
-    others = (at(X + nx - 1, 1 - k), at(X + 1, 1 - k), at(X + 2, 1 - k), at(X, 1 - k))
+    packet = lambda xx: k * nx + lax.rem(xx, nx)
+    own, pL, pR, pO = packet(X), packet(X + nx - 1), packet(X + 1), packet(X + 2)
     par = lax.rem(y, 2)
     mine, other = par * HR, (1 - par) * HR
 
@@ -64,6 +65,12 @@
         return pl.ds(pl.multiple_of(base + q * QR, QR), QR)
 
     PARTS = {None: pl.ds(0, 3), 0: pl.ds(0, 2), 1: pl.ds(2, 1)}
+
+    def home(n):
+        return wbuf.at[n] if n < 2 else G.at[n]
+
+    def kept(n):
+        return pltpu.make_async_copy(wbuf.at[n], G.at[n], w_sem.at[n, 0])
 
     def out_copy(t, n, part=None):
         full = pl.ds(0, DR)
@@ -77,8 +84,8 @@
         }
         j, r, who = spec[t]
         q = PARTS[part]
-        src = own_v.at[lax.rem(n, 4), q, r, :] if j is None else G.at[n, q, j, r, :]
-        dst = G.at[n, q, s if j is None else j, r, :]
+        src = own_v.at[lax.rem(n, 4), q, r, :] if j is None else home(n).at[q, j, r, :]
+        dst = home(n).at[q, own if j is None else j, r, :]
         leaves = g_send.at[lax.rem(n, 4), 0 if j is None else 1]
         return remote(src, dst, leaves, g_recv.at[8 if part == 1 else lax.rem(n, 8), STAGE[t]], who)
 
@@ -155,7 +162,7 @@
         own_down(n, own_sem.at[lax.rem(n, 4)])
 
     def own_stored(n):
-        return pltpu.make_async_copy(own_v.at[lax.rem(n, 4)], G.at[n, :, s], own_out.at[lax.rem(n, 4)])
+        return pltpu.make_async_copy(own_v.at[lax.rem(n, 4)], home(n).at[:, own], own_out.at[lax.rem(n, 4)])
 
     @stage
     def gA(n):
@@ -166,7 +173,7 @@
 
     @stage
     def gB(n, part=None):
-        when(n >= 4, lambda: left_passed(n - 4))
+        when(n >= 6, lambda: left_passed(n - 4))
         in_wait(0, n, part)
         starts(n, part, 4, 5, 6, 10)
 
@@ -187,34 +194,44 @@
         if part != 1:
             own_stored(n).wait()
 
-    def load(n, packets, *parts):
-        slot = lax.rem(n, 2)
+    def lane(core):
+        return pl.ds(pl.multiple_of(core * nx, nx), nx)
+
+    def load(n, slot, lanes, *parts):
         for part in parts:
-            q = PARTS[part]
-            for p in packets:
-                pltpu.make_async_copy(G.at[n, q, p], wbuf.at[slot, q, p], w_sem.at[slot, part]).start()
+            for core in lanes:
+                at_ = (PARTS[part], lane(core))
+                pltpu.make_async_copy(G.at[n, *at_], wbuf.at[slot, *at_], w_sem.at[slot, part]).start()
 
     def wait_weights(slot, part):
         to = wbuf.at[slot, PARTS[part]]
         pltpu.make_async_copy(to, to, w_sem.at[slot, part]).wait()
 
     @stage
-    def gL(n, *parts):
-        load(n, (s, pL, pR, pO), *(parts or (0, 1)))
+    def gL(n):
+        if isinstance(n, int) and n in (2, 3):
+            left_passed(n - 2)
+            kept(n - 2).wait()
+        load(n, lax.rem(n, 2), (k,), 0, 1)
 
     @stage
     def gF(n, part=None):
         in_wait(4, n, part)
-        load(n, others, *((0, 1) if part is None else (part,)))
-
-    def w_cols(slot, q):
-        return wbuf[slot, q].reshape(D, CW)
+        if isinstance(n, int) and n < 2:
+            if part != 0:
+                kept(n).start()
+        else:
+            load(n, lax.rem(n, 2), (1 - k,), 0, 1)
+
+    def w_cols(slot, q, n):
+        cols = pl.ds(n * NH, NH)
+        return jnp.concatenate([wbuf[slot, q, c * nx + x, :, cols] for x in range(nx) for c in range(CORES)], axis=0)
 
     def w_half(slot, q, h):
-        return wbuf[slot, q, pl.ds(h * nx, nx)].reshape(DH, CW)
+        return jnp.concatenate([wbuf[slot, q, c * nx + h * (nx // 2) + x] for x in range(nx // 2) for c in range(CORES)], axis=0)
 
     def wd_half(slot, h):
-        return jnp.concatenate([wbuf[slot, D_, CORES * j + h] for j in range(nx)], axis=0)
+        return wbuf[slot, D_, pl.ds(h * nx, nx)].reshape(CW, DH)
 
     def tile(i, n=None):
         n = TM if n is None else n
@@ -420,8 +437,7 @@
     def both(ref, r):
         return jnp.concatenate([ref[0, r, :], ref[1, r, :]], axis=1)
 
-    def put_a(h, i):
-        r = tile(i, TN)
+    def put_a(h, r):
         scale = lax.rsqrt(jnp.mean(h * h, -1, keepdims=True) + 1e-6)
         a = (h * scale).astype(BF)
         a_nat[r, :] = a
@@ -429,7 +445,7 @@
 
     def norm0(i, _):
         r = tile(i, TN)
-        put_a(both(dyv, r).astype(F32), i)
+        put_a(both(dyv, r).astype(F32), r)
         acc[r, :] = jnp.zeros((TN, D), F32)
         return _
 
@@ -444,31 +460,28 @@
     gB(0, 0)
     gC(0, 0)
     gB(0, 1)
+    gA(1)
     gC(0, 1)
-    gA(1)
     exchanged(1)
     gS(2)
     gD(0, 0)
     gD(0, 1)
+    gE(0, 0)
     gB(1)
     gA(2)
     gS(3)
-    gE(0, 0)
-    gL(0, 0)
-    gC(1)
     gE(0, 1)
-    gL(0, 1)
     gF(0, 0)
 
     A, B, C_, D__, E, F, L = gA, gB, gC, gD, gE, gF, gL
     fwd_hooks = {
-        (0, 0): [(F, 0, 1), (D__, 1), (B, 2)], (0, 1): [(C_, 2), (A, 3)], (0, 2): [(E, 1), (L, 1), (D__, 2)], (0, 3): [(B, 3), (F, 1)],
-        (1, 0): [(C_, 3), (E, 2), (L, 2), (A, 4)], (1, 1): [(D__, 3)], (1, 2): [(F, 2), (B, 4)], (1, 3): [(C_, 4), (E, 3), (A, 5)],
-        (2, 0): [(L, 3)], (2, 1): [(D__, 4)], (2, 2): [(F, 3), (B, 5)], (2, 3): [(C_, 5), (E, 4), (A, 6)],
-        (3, 0): [(L, 4)], (3, 1): [(D__, 5)], (3, 2): [(F, 4), (B, 6)], (3, 3): [(C_, 6), (E, 5), (A, 7)],
-        (4, 0): [(L, 5)], (4, 1): [(D__, 6)], (4, 2): [(F, 5), (B, 7)], (4, 3): [(C_, 7), (E, 6), (A, 8)],
-        (5, 0): [(L, 6)], (5, 1): [(D__, 7)], (5, 2): [(F, 6), (B, 8)], (5, 3): [(C_, 8), (E, 7), (A, 9)],
-        (6, 0): [(L, 7)], (6, 1): [(D__, 8)], (6, 2): [(F, 7), (B, 9)], (6, 3): [(C_, 9), (E, 8), (A, 10)],
+        (0, 0): [(C_, 1), (F, 0, 1)], (0, 1): [(D__, 1), (B, 2), (A, 3)], (0, 2): [(C_, 2), (E, 1)], (0, 3): [(D__, 2), (F, 1)],
+        (1, 0): [(B, 3), (A, 4)], (1, 1): [(C_, 3), (E, 2), (L, 2)], (1, 2): [(D__, 3), (B, 4), (F, 2), (A, 5)], (1, 3): [(C_, 4)],
+        (2, 1): [(E, 3), (L, 3), (D__, 4)], (2, 2): [(B, 5), (C_, 5), (F, 3), (A, 6)], (2, 3): [(E, 4)],
+        (3, 0): [(L, 4)], (3, 1): [(D__, 5)], (3, 2): [(F, 4), (B, 6), (C_, 6), (A, 7)], (3, 3): [(E, 5)],
+        (4, 0): [(L, 5)], (4, 1): [(D__, 6)], (4, 2): [(F, 5), (B, 7), (A, 8)], (4, 3): [(C_, 7), (E, 6)],
+        (5, 0): [(L, 6)], (5, 1): [(D__, 7)], (5, 2): [(F, 6), (B, 8), (A, 9)], (5, 3): [(C_, 8), (E, 7)],
+        (6, 0): [(L, 7)], (6, 1): [(D__, 8)], (6, 2): [(F, 7), (B, 9), (A, 10)], (6, 3): [(C_, 9), (E, 8)],
     }
 
     def fwd_hook(h, c):
@@ -489,20 +502,20 @@
         cols = tile(i)
         return pltpu.make_async_copy(pt.at[:, :, cols], PT.at[c, :, :, cols], pt_sem.at[i])
 
-    def gate_up(slot, r):
+    def gate_up(slot, r, n):
         a = a_nat[r, :]
-        g, u = dot(a, w_cols(slot, G_)), dot(a, w_cols(slot, U_))
+        g, u = dot(a, w_cols(slot, G_, n)), dot(a, w_cols(slot, U_, n))
         sig = jax.nn.sigmoid(g)
         silu = g * sig
         return silu, u * (sig + silu * (1.0 - sig)), (silu * u).astype(BF)
 
-    def put_pt(p, i):
-        pt[:, :, tile(i, TM // SUB)] = p.T.reshape(nx, BW, TM // SUB)
+    def put_pt(p, i, n):
+        nb = NH // BW
+        pt[n * nb:(n + 1) * nb, :, tile(i, TM // SUB)] = p.T.reshape(nb, BW, TM // SUB)
 
     def fwd(c, carry):
         slot = lax.rem(c, 2)
-        wait_weights(slot, 0)
-
+        pl.when(c >= 2)(lambda: wait_weights(slot, 0))
         fwd_hook(0, c)
 
         def up_tile(i, _):
@@ -517,19 +530,21 @@
                 for j in range(SUB):
                     e = SUB * i + j
                     r = tile(e, TM // SUB)
-                    silu, slope, p = gate_up(slot, r)
                     inner = pl.ds(j * (TM // SUB), TM // SUB)
-                    stb[i, 0, inner] = silu
-                    stb[i, 1, inner] = slope
-                    put_pt(p, e)
-                    dgu[0, r, :] = p
+                    for n in range(CW // NH):
+                        cols = pl.ds(n * NH, NH)
+                        silu, slope, p = gate_up(slot, r, n)
+                        stb[i, 0, inner, cols] = silu
+                        stb[i, 1, inner, cols] = slope
+                        put_pt(p, e, n)
+                        dgu[0, r, cols] = p
             st_out(TILES * c + i).start()
             pt_out(c, i).start()
             return _
 
         lax.fori_loop(0, TILES, up_tile, 0)
         fwd_hook(2, c)
-        wait_weights(slot, 1)
+        pl.when(c >= 2)(lambda: wait_weights(slot, 1))
 
         @pl.when(c < C - 1)
         def _():
@@ -543,23 +558,22 @@
 
             def one(j, _):
                 with jax.named_scope("fwd_last"):
-                    for e in range(NT // 2):
-                        i = NT // 2 * j + e
-                        r = tile(i, TN)
+                    for e in range(NT // 4):
+                        r = tile(NT // 4 * j + e, TN)
                         total = acc[r, :] + jnp.concatenate([dot(dgu[0, r, :], wd_half(slot, h)) for h in range(2)], axis=1)
                         h = (both(dyv, r).astype(F32) + total.astype(BF).astype(F32)).astype(BF)
                         for g in range(2):
                             dgu[g, r, :] = h[:, g * DH:(g + 1) * DH]
-                        put_a(h.astype(F32), i)
+                        put_a(h.astype(F32), r)
                         acc[r, :] = jnp.zeros((TN, D), F32)
-                r = tile(j, T // 2)
+                r = tile(j, T // 4)
                 for g in range(2):
                     pltpu.make_async_copy(dgu.at[g, r], H1.at[g, r], ld_sem.at[2]).start()
                 for c_ in halves(dy_ref.at[0], dyv, r, ld_sem.at[0]):
                     c_.start()
                 return _
 
-            lax.fori_loop(0, 2, one, 0)
+            lax.fori_loop(0, 4, one, 0)
 
         fwd_hook(3, c)
         return carry
@@ -571,12 +585,14 @@
     pltpu.make_async_copy(dgu, H1, ld_sem.at[2]).wait()
     pltpu.make_async_copy(dyv, dyv, ld_sem.at[0]).wait()
 
-    def d_p(slot, r):
-        return dot(dyv[0, r, :], wd_half(slot, 0), 1, 1) + dot(dyv[1, r, :], wd_half(slot, 1), 1, 1)
-
-    def put_d(r, dp, silu, slope):
-        dgu[G_, r, :] = (dp * slope).astype(BF)
-        dgu[U_, r, :] = (dp * silu).astype(BF)
+    def d_p(slot, r, n):
+        blocks = lambda h: wbuf[slot, D_, pl.ds(h * nx + n * (NH // BW), NH // BW)].reshape(NH, DH)
+        return dot(dyv[0, r, :], blocks(0), 1, 1) + dot(dyv[1, r, :], blocks(1), 1, 1)
+
+    def put_d(r, n, dp, silu, slope):
+        cols = pl.ds(n * NH, NH)
+        dgu[G_, r, cols] = (dp * slope).astype(BF)
+        dgu[U_, r, cols] = (dp * silu).astype(BF)
 
     h1_in = [pltpu.make_async_copy(H1.at[h], a_nat.at[:, pl.ds(h * DH, DH)], ld_sem.at[0]) for h in range(2)]
     a0t_in = pltpu.make_async_copy(A0T, a_t, ld_sem.at[1])
@@ -598,16 +614,18 @@
         along = jnp.sum(d * h, -1, keepdims=True) * (scale * scale * scale) * (1.0 / D)
         return (through + (d * scale - h * along)).astype(BF)
 
+    def mid_tile(r):
+        out = norm_back(a_nat[r, :].astype(F32), acc[r, :], both(dyv, r).astype(F32))
+        for e in range(2):
+            dyv[e, r, :] = out[:, e * DH:(e + 1) * DH]
+        acc[r, :] = jnp.zeros((TN, D), F32)
+
     def middle():
         pltpu.make_async_copy(a_nat, a_nat, ld_sem.at[0]).wait()
 
         def mid(i, _):
             with jax.named_scope("mid"):
-                r = tile(i, TN)
-                out = norm_back(a_nat[r, :].astype(F32), acc[r, :], both(dyv, r).astype(F32))
-                for e in range(2):
-                    dyv[e, r, :] = out[:, e * DH:(e + 1) * DH]
-                acc[r, :] = jnp.zeros((TN, D), F32)
+                mid_tile(tile(i, TN))
             return _
 
         lax.fori_loop(0, NT, mid, 0)
@@ -647,7 +665,7 @@
 
         @pl.when(first_layer & (m < 2 * C - 1))
         def _():
-            load(m + 1 - C, range(CORES * nx), 0, 1)
+            load(m + 1 - C, 1 - slot, range(CORES), 0, 1)
 
         hook(0, m)
 
@@ -658,9 +676,10 @@
             with jax.named_scope("bwd1_tile"):
                 for e in range(TILES * SUB):
                     r = tile(e, TM // SUB)
-                    silu, slope, p = gate_up(slot, r)
-                    put_pt(p, e)
-                    put_d(r, d_p(slot, r), silu, slope)
+                    for n in range(CW // NH):
+                        silu, slope, p = gate_up(slot, r, n)
+                        put_pt(p, e, n)
+                        put_d(r, n, d_p(slot, r, n), silu, slope)
 
         @pl.when(first_layer)
         def _():
@@ -671,7 +690,9 @@
                 for e in range(TILES * SUB):
                     r = pl.ds(e * (TM // SUB), TM // SUB)
                     inner = pl.ds((e % SUB) * (TM // SUB), TM // SUB)
-                    put_d(r, d_p(slot, r), stb[e // SUB, 0, inner], stb[e // SUB, 1, inner])
+                    for n in range(CW // NH):
+                        cols = pl.ds(n * NH, NH)
+                        put_d(r, n, d_p(slot, r, n), stb[e // SUB, 0, inner, cols], stb[e // SUB, 1, inner, cols])
             pl.when(m < 2 * C - 1)(lambda: dg_out(m - C).start())
             pt_in(m - C).wait()
 
@@ -682,7 +703,7 @@
         def _():
             for c_ in h1_in:
                 c_.start()
-            load(0, range(CORES * nx), 0, 1)
+            load(0, 0, range(CORES), 0, 1)
 
         @pl.when((m >= C - 1) & (m < 2 * C - 1))
         def _():
@@ -726,8 +747,7 @@
 
         @pl.when(j < C - 1)
         def _():
-            for p in range(CORES * nx):
-                pltpu.make_async_copy(G.at[j, PARTS[0], p], wbuf.at[1 - slot, PARTS[0], p], w_sem.at[1 - slot, 0]).start()
+            load(j, 1 - slot, range(CORES), 0)
             dg_in(j, 1 - half).start()
 
         d_a(slot, T // 2, pl.multiple_of(half * (T // 2), T // 2))

time: 370 us -> 365 us (0.986)
  Pallas kernels: 360 us -> 356 us
    pallas_call x1, Pallas kernels: 360 us -> 356 us  [step(): pl.pallas_call(functools.partial(kernel, (nx, ny, C, T, D)), out_shape=[s...]
where the time goes in v4:
time: 365 us
  Pallas kernels  356 us (98%)
  local copies, waits for them, and re-layouts  8.51 us (2%)
    pallas_call x1, Pallas kernels, step(): pl.pallas_call(functools.partial(kernel, (nx, ny, C, T, D)), out_shape=[s...  356 us
    unnamed x10, local copies, waits for them, and re-layouts  8.51 us

profile of v4, /device:TPU:97, one launch (start us, length us, event | category | flops | bytes accessed | tf_op | source)
XLA Modules:
  0.0 365.0 jit_solution(14120407419102604018)
XLA Ops:
  0.6 355.8 %stack.1 = (bf16[1,2048,1024]{2,1,0:T(8,128)(2,1)}, bf16[2,128,3584]{2,1,0:T(8,128)(2,1)}, bf16[2,128,3584]{2,1,0:T(8,128)(2,1)}, bf16[2,448,1024]{2,1,0:T(8,128...) custom-call(bf16[1,2048,1024]{2,1,0:T(8,128)(2,1)} %x_ref.1, ...), custom_call_target="tpu_custom_call" | custom-call | tf_op jit(solution)/shard_map/stack/pallas_call | solution.py:806
  356.5 0.0 copy-start.2
  356.5 0.0 copy-start.1
  356.5 4.8 %copy.13 = bf16[1,2048,1024]{2,1,0:T(8,128)(2,1)} copy(bf16[1,2048,1024]{2,1,0:T(8,128)(2,1)} %get-tuple-element.16) | data formatting | bytes 8388608
  361.3 0.0 copy-done.2
  361.3 0.0 copy-start
  361.3 1.2 copy.14
  362.5 0.0 copy-done.1
  362.5 1.2 copy.15
  363.8 0.0 copy-done
  363.8 1.2 copy.16
Async XLA Ops:
  356.5 4.8 %copy-start.2 = (bf16[2,128,3584]{2,1,0:T(8,128)(2,1)S(1)}, bf16[2,128,3584]{2,1,0:T(8,128)(2,1)}, u32[]{:S(2)}) copy-start(bf16[2,128,3584]{2,1,0:T(8,128)(2,1)} %get-tuple-element.17) | copy-start | bytes 5505028
  356.5 6.1 %copy-start.1 = (bf16[2,128,3584]{2,1,0:T(8,128)(2,1)S(1)}, bf16[2,128,3584]{2,1,0:T(8,128)(2,1)}, u32[]{:S(2)}) copy-start(bf16[2,128,3584]{2,1,0:T(8,128)(2,1)} %get-tuple-element.18) | copy-start | bytes 5505028
  361.3 2.5 copy-start

commit v5 on v4

--- a/solution.py
+++ b/solution.py
@@ -281,17 +281,18 @@
         }[t]
         return remote(src, dst, rs_send.at[1 if t < 4 else 2], sem, who)
 
+    turn = jnp.where(par == 0, 1, ny - 1)
+    first_pair, second_pair = {"r": lax.rem(y + turn, ny)}, {"r": lax.rem(y + ny - turn, ny)}
+
     def y_copy(t, m):
         three = lax.rem(m, 3)
         src, dst, who = {
-            0: (v.at[three, :, lo], ya.at[three, :, lo], up),
-            1: (v.at[three, :, hi], ya.at[three, :, hi], up),
-            2: (v.at[three, :, hi], yb.at[three, :, hi], down),
-            3: (v.at[three, :, lo], yb.at[three, :, lo], down),
-            4: (ya.at[three, :, lo], yc.at[three, :, lo], up),
-            5: (yb.at[three, :, hi], yc.at[three, :, hi], down),
+            0: (v.at[three, :, lo], ya.at[three, :, lo], first_pair),
+            1: (v.at[three, :, hi], ya.at[three, :, hi], second_pair),
+            2: (yb.at[three, :, lo], yc.at[three, :, lo], second_pair),
+            3: (yb.at[three, :, hi], yc.at[three, :, hi], first_pair),
         }[t]
-        return remote(src, dst, ys_sem.at[three], yr_sem.at[three, 0 if t in (0, 2) else 1], who)
+        return remote(src, dst, ys_sem.at[three], yr_sem.at[three, t // 2], who)
 
     @named
     def keep_lanes(m):
@@ -345,14 +346,17 @@
         two, three = lax.rem(m, 2), lax.rem(m, 3)
         for q in range(3):
             v[three, q] = (own32[two, q] + rc[three, q].astype(F32) + rd[three, q].astype(F32)).astype(BF)
-        for t in (0, 2, 1, 3):
+        for t in (0, 1):
             y_copy(t, m).start()
 
     @named
     def y2(m):
-        arrived(one, yr_sem.at[lax.rem(m, 3), 0])
-        y_copy(4, m).start()
-        y_copy(5, m).start()
+        three = lax.rem(m, 3)
+        arrived(one, yr_sem.at[three, 0])
+        for q in range(3):
+            yb[three, q] = (v[three, q].astype(F32) + ya[three, q].astype(F32)).astype(BF)
+        for t in (2, 3):
+            y_copy(t, m).start()
 
     def where_m(m):
         first = m < C
@@ -379,19 +383,17 @@
 
     @named
     def y3_wait(m):
-        arrived(two_, yr_sem.at[lax.rem(m, 3), 1])
+        arrived(one, yr_sem.at[lax.rem(m, 3), 1])
         when(m > 0, lambda: out_done(m - 1))
 
     def y3_add(m):
         three = slot_of(m, 3)
         for q in range(3):
-            a = v[three, q].astype(F32) + yc[three, q].astype(F32)
-            b = ya[three, q].astype(F32) + yb[three, q].astype(F32)
-            f_out[q] = (a + b).astype(BF)
+            f_out[q] = (yb[three, q].astype(F32) + yc[three, q].astype(F32)).astype(BF)
 
     @named
     def y3_out(m):
-        arrived(v, ys_sem.at[lax.rem(m, 3)])
+        arrived(two_, ys_sem.at[lax.rem(m, 3)])
         for q in (G_, U_):
             for c_ in cols_out(q, m):
                 c_.start()
@@ -466,10 +468,10 @@
     gS(2)
     gD(0, 0)
     gD(0, 1)
-    gE(0, 0)
     gB(1)
     gA(2)
     gS(3)
+    gE(0, 0)
     gE(0, 1)
     gF(0, 0)
 
@@ -549,8 +551,10 @@
         @pl.when(c < C - 1)
         def _():
             with jax.named_scope("fwd_down"):
-                for h in range(2):
-                    acc[:, h * DH:(h + 1) * DH] += dot(dgu[0], wd_half(slot, h))
+                for e in range(2):
+                    r = pl.ds(e * (T // 2), T // 2)
+                    for h in range(2):
+                        acc[r, h * DH:(h + 1) * DH] += dot(dgu[0, r, :], wd_half(slot, h))
 
         @pl.when(c == C - 1)
         def _():
@@ -633,8 +637,8 @@
         a0t_in.wait()
 
     at_hook = {
-        0: {0: [(gD, 2), (gA, 4), (gS, 5)], 1: [(gD, 4), (gB, 5), (gC, 5), (gE, 3), (gA, 6)], 2: [(gB, 6), (gC, 6)], 3: [(gE, 6)]},
-        2: {0: [(gB, 3), (gC, 3), (gE, 2), (gB, 4), (gC, 4), (gA, 5), (gS, 6)], 1: [(gE, 4)], 2: [(gE, 5)]},
+        0: {0: [(gD, 2), (gA, 4), (gS, 5)], 1: [(gD, 4), (gB, 5), (gC, 5), (gE, 3), (gA, 6)], 2: [(gB, 6), (gC, 6)]},
+        2: {0: [(gB, 3), (gC, 3), (gE, 2), (gB, 4), (gC, 4), (gA, 5), (gS, 6)], 1: [(gE, 4)], 2: [(gE, 5)], 3: [(gE, 6)]},
         3: {},
         4: {0: [(gD, 3)], 1: [(gD, 5)], 2: [(gD, 6)]},
     }

time: 365 us -> 360 us (0.986)
  Pallas kernels: 356 us -> 350 us
    pallas_call x1, Pallas kernels: 356 us -> 350 us  [step(): pl.pallas_call(functools.partial(kernel, (nx, ny, C, T, D)), out_shape=[s...]
where the time goes in v5:
time: 360 us
  Pallas kernels  350 us (97%)
  local copies, waits for them, and re-layouts  8.51 us (2%)
    pallas_call x1, Pallas kernels, step(): pl.pallas_call(functools.partial(kernel, (nx, ny, C, T, D)), out_shape=[s...  350 us
    unnamed x10, local copies, waits for them, and re-layouts  8.51 us

profile of v5, /device:TPU:97, one launch (start us, length us, event | category | flops | bytes accessed | tf_op | source)
XLA Modules:
  0.0 359.6 jit_solution(10476180838668447585)
XLA Ops:
  0.6 350.5 %stack.1 = (bf16[1,2048,1024]{2,1,0:T(8,128)(2,1)}, bf16[2,128,3584]{2,1,0:T(8,128)(2,1)}, bf16[2,128,3584]{2,1,0:T(8,128)(2,1)}, bf16[2,448,1024]{2,1,0:T(8,128...) custom-call(bf16[1,2048,1024]{2,1,0:T(8,128)(2,1)} %x_ref.1, ...), custom_call_target="tpu_custom_call" | custom-call | tf_op jit(solution)/shard_map/stack/pallas_call | solution.py:810
  351.1 0.0 copy-start.2
  351.1 0.0 copy-start.1
  351.1 4.8 %copy.13 = bf16[1,2048,1024]{2,1,0:T(8,128)(2,1)} copy(bf16[1,2048,1024]{2,1,0:T(8,128)(2,1)} %get-tuple-element.16) | data formatting | bytes 8388608
  355.9 0.0 copy-done.2
  355.9 0.0 copy-start
  355.9 1.2 copy.14
  357.2 0.0 copy-done.1
  357.2 1.2 copy.15
  358.4 0.0 copy-done
  358.4 1.2 copy.16
Async XLA Ops:
  351.1 4.8 %copy-start.2 = (bf16[2,128,3584]{2,1,0:T(8,128)(2,1)S(1)}, bf16[2,128,3584]{2,1,0:T(8,128)(2,1)}, u32[]{:S(2)}) copy-start(bf16[2,128,3584]{2,1,0:T(8,128)(2,1)} %get-tuple-element.17) | copy-start | bytes 5505028
  351.1 6.1 %copy-start.1 = (bf16[2,128,3584]{2,1,0:T(8,128)(2,1)S(1)}, bf16[2,128,3584]{2,1,0:T(8,128)(2,1)}, u32[]{:S(2)}) copy-start(bf16[2,128,3584]{2,1,0:T(8,128)(2,1)} %get-tuple-element.18) | copy-start | bytes 5505028
  355.9 2.5 copy-start
